TPU v7x, 128 devices: a whole 4x4x4 slice. The times are simulated.
128 devices in a mesh: gossip: 32 (over z, y_lo, x), mp: 4 (over y_hi, core).
Axes of the slice: x: 4, y: 4 (y_hi: 2, y_lo: 2; y = y_hi * 2 + y_lo), z: 4, core: 2. Of those that a mesh axis runs over, the one named last changes fastest.
Arguments:
- tokens: bfloat16 [32, 512, 2048], P('gossip'), may hold values from -6 to 6
- targets: bfloat16 [32, 512, 2048], P('gossip'), may hold values from -6 to 6
- gate_weight: bfloat16 [32, 2048, 4096], P('gossip', None, 'mp'), may hold values from -6 to 6
- up_weight: bfloat16 [32, 2048, 4096], P('gossip', None, 'mp'), may hold values from -6 to 6
- down_weight: bfloat16 [32, 4096, 2048], P('gossip', 'mp'), may hold values from -6 to 6
Outputs:
- gate_out: bfloat16 [32, 2048, 4096], P('gossip', None, 'mp')
- up_out: bfloat16 [32, 2048, 4096], P('gossip', None, 'mp')
- down_out: bfloat16 [32, 4096, 2048], P('gossip', 'mp')
All inputs are finite; a program needn't handle non-finite values.
Results may differ from a plain program's by a relative error of at most 0.0095.
Values may be sent and summed in bfloat16 or wider, within the bound.
No kernel may reach another device: no remote copies, remote signals or barrier semaphores. Data moves between devices by JAX's collectives and lax.ppermute only.
A program may use at most 128 MiB of HBM per device.

v0:
```python
import jax
import jax.numpy as jnp
from jax import lax
from jax.sharding import PartitionSpec as P

ITERS = 1


def passed_along(value, axis, steps):
    count = lax.axis_size(axis)
    pairs = [(source, (source + steps) % count) for source in range(count)]
    return lax.ppermute(value, axis, pairs)


def rms_norm(values):
    widened = values.astype(jnp.float32)
    return (
        widened * lax.rsqrt(jnp.mean(widened * widened, axis=-1, keepdims=True) + 1e-06)
    ).astype(jnp.bfloat16)


def mix_three(lower, own, upper):
    total = lower.astype(jnp.float32) + own.astype(jnp.float32) + upper.astype(jnp.float32)
    return (total / 3.0).astype(jnp.bfloat16)


def local(tokens, targets, gate_weight, up_weight, down_weight):
    inputs = tokens[0]
    wanted = targets[0]
    w_gate = gate_weight[0]
    w_up = up_weight[0]
    w_down = down_weight[0]
    tok_count = inputs.shape[0]
    width = inputs.shape[1]
    mp_count = lax.axis_size("mp")
    hidden_all = w_gate.shape[1] * mp_count
    in_scale = 1.0 / width**0.5
    mid_scale = 1.0 / hidden_all**0.5
    step_size = hidden_all / 4.0
    normed = rms_norm(inputs)
    offset = inputs.astype(jnp.float32) - wanted.astype(jnp.float32)
    own_rows = tok_count // mp_count
    offset_own = lax.dynamic_slice_in_dim(offset, lax.axis_index("mp") * own_rows, own_rows, 0)
    for iteration in range(ITERS):
        gate_pre = jnp.dot(normed, w_gate, preferred_element_type=jnp.float32) * in_scale
        up_pre = jnp.dot(normed, w_up, preferred_element_type=jnp.float32) * in_scale
        sig_gate = jax.nn.sigmoid(gate_pre)
        act_gate = gate_pre * sig_gate
        hidden = (act_gate * up_pre).astype(jnp.bfloat16)
        partial_value = jnp.dot(hidden, w_down, preferred_element_type=jnp.float32)
        output_own = (
            lax.psum_scatter(
                partial_value.astype(jnp.bfloat16), "mp", scatter_dimension=0, tiled=True
            ).astype(jnp.float32)
            * mid_scale
        )
        err_own = ((offset_own + output_own) / tok_count).astype(jnp.bfloat16)
        err_grad = lax.all_gather(err_own, "mp", axis=0, tiled=True)
        grad_down = (
            jnp.einsum("tf,td->fd", hidden, err_grad, preferred_element_type=jnp.float32)
            * mid_scale
        )
        new_down = (w_down.astype(jnp.float32) - step_size * grad_down).astype(jnp.bfloat16)
        down_low = passed_along(new_down, "gossip", 1)
        down_high = passed_along(new_down, "gossip", -1)
        grad_hidden = (
            jnp.einsum("td,fd->tf", err_grad, w_down, preferred_element_type=jnp.float32)
            * mid_scale
        )
        grad_gate = (
            grad_hidden * up_pre * (sig_gate * (1.0 + gate_pre * (1.0 - sig_gate)))
        ).astype(jnp.bfloat16)
        grad_up = (grad_hidden * act_gate).astype(jnp.bfloat16)
        grad_wgate = (
            jnp.einsum("td,tf->df", normed, grad_gate, preferred_element_type=jnp.float32)
            * in_scale
        )
        grad_wup = (
            jnp.einsum("td,tf->df", normed, grad_up, preferred_element_type=jnp.float32) * in_scale
        )
        new_gate = (w_gate.astype(jnp.float32) - step_size * grad_wgate).astype(jnp.bfloat16)
        new_up = (w_up.astype(jnp.float32) - step_size * grad_wup).astype(jnp.bfloat16)
        inner = jnp.stack([new_gate, new_up])
        inner_low = passed_along(inner, "gossip", 1)
        inner_high = passed_along(inner, "gossip", -1)
        inner_mixed = mix_three(inner_low, inner, inner_high)
        w_gate = inner_mixed[0]
        w_up = inner_mixed[1]
        w_down = mix_three(down_low, new_down, down_high)
    return (w_gate[None], w_up[None], w_down[None])


def solution(mesh):
    placed = (
        P("gossip", None, None),
        P("gossip", None, None),
        P("gossip", None, "mp"),
        P("gossip", None, "mp"),
        P("gossip", "mp", None),
    )
    return jax.shard_map(
        local,
        mesh=mesh,
        in_specs=placed,
        out_specs=(P("gossip", None, "mp"), P("gossip", None, "mp"), P("gossip", "mp", None)),
        check_vma=False,
    )
```

profile of v0, /device:TPU:0, one launch (start us, length us, event | category | flops | bytes accessed | tf_op | source)
XLA Modules:
  0.0 425.0 jit_solution(3292398702142443393)
XLA Ops:
  7.2 0.0 reduce-scatter.2.cloned.1.call-start
  7.2 2.1 multiply_reduce_fusion
  9.3 5.3 %fusion.8 = f32[512,1024]{1,0:T(8,128)S(1)} fusion(bf16[1,2048,1024]{2,1,0:T(8,128)(2,1)} %param.7, bf16[1,512,2048]{2,1,0:T(8,128)(2,1)} %param.5, f32[512]{0:T(512)S(1)} %add_rsqrt_fusion), kind=kOutput, calls=%fused_computation.16 | convolution fusion | flops 2150629376 | bytes 8390656 | tf_op jit(solution)/shard_map/dot_general | solution.py:45
  14.7 4.0 multiply_convert_fusion.5
  18.7 1.0 copy-done.11
  19.7 3.7 fusion.12
  23.4 0.2 all-gather.2.cloned.1.call-start
  23.6 2.5 convert_bitcast_fusion
  26.2 38.1 %reduce-scatter.2.cloned.1.call-done = bf16[128,2048]{1,0:T(8,128)(2,1)} async-done(((bf16[512,2048]{1,0:T(8,128)(2,1)}), bf16[128,2048]{1,0:T(8,128)(2,1)}) %reduce-scatter.2.cloned.1.call-update) | async-done | bytes 524304 | tf_op jit(solution)/shard_map/reduce_scatter | solution.py:52
  64.3 2.5 fusion.19
  66.8 26.3 %all-gather.2.cloned.1.call-done = bf16[512,2048]{1,0:T(8,128)(2,1)} async-done(((bf16[128,2048]{1,0:T(8,128)(2,1)}), bf16[512,2048]{1,0:T(8,128)(2,1)}) %all-gather.2.cloned.1.call-update) | async-done | bytes 2097168 | tf_op jit(solution)/shard_map/all_gather | solution.py:58
  93.1 5.3 %fusion.2 = f32[512,1024]{1,0:T(8,128)S(1)} fusion(bf16[512,2048]{1,0:T(8,128)(2,1)} %all-gather.2.cloned.1.call-done, bf16[1,1024,2048]{2,1,0:T(8,128)(2,1)} %param.9), kind=kOutput, calls=%fused_computation.10 | convolution fusion | flops 2147483648 | bytes 8388608 | tf_op jit(solution)/shard_map/td,fd->tf/dot_general | solution.py:67
  98.5 3.1 fusion.11
  101.6 4.8 %fusion.10 = bf16[1,2048,1024]{2,1,0:T(8,128)(2,1)} fusion(bf16[1,2048,1024]{2,1,0:T(8,128)(2,1)S(1)} %copy-done.6, f32[512,1024]{1,0:T(8,128)S(1)} %fusion.2, f32[512,1024]{1,0:T(8,128)S(1)} %copy-done.12, f32[512,1024]{1,0:T(8,128)S(1)} %copy-done.10, bf16[1,512,2048]{2,1,0:T(8,128)(2,1)S(1)} %copy-done.1, f32[512]{0:T(512)S(1)} %add_rsqrt_fusion), kind=kOutput, calls=%fused_computation.20 | convolution fusion | flops 2165833728 | bytes 16779264 | tf_op jit(solution)/shard_map/td,tf->df/dot_general | solution.py:75
  106.4 6.3 %pad_maximum_fusion = bf16[2,2048,1024]{2,1,0:T(8,128)(2,1)} fusion(bf16[1,2048,1024]{2,1,0:T(8,128)(2,1)S(1)} %fusion.11, bf16[1,2048,1024]{2,1,0:T(8,128)(2,1)} %fusion.10), kind=kLoop, calls=%fused_computation.1 | loop fusion | flops 4194304 | bytes 16777216 | tf_op jit(solution)/shard_map/stack | solution.py:83
  112.8 5.1 %collective-permute-start.1 = (bf16[2,2048,1024]{2,1,0:T(8,128)(2,1)}, bf16[2,2048,1024]{2,1,0:T(8,128)(2,1)}, u32[]{:S(2)}, u32[]{:S(2)}) collective-permute-start(bf16[2,2048,1024]{2,1,0:T(8,128)(2,1)} %pad_maximum_fusion), channel_id=1, source_target_pairs={{0,124},{4,0},{8,4},{12,8},{16,12},{20,16},{24,20},{28,24},{32,28}... | collective-permute-start | bytes 25165832 | tf_op jit(solution)/shard_map/ppermute | solution.py:12
  117.9 5.0 %subtract_convert_fusion = bf16[1024,2048]{1,0:T(8,128)(2,1)S(1)} fusion(bf16[512,1024]{1,0:T(8,128)(2,1)} %copy-done.11, bf16[512,2048]{1,0:T(8,128)(2,1)S(1)} %copy-done.8, bf16[1,1024,2048]{2,1,0:T(8,128)(2,1)} %param.9), kind=kOutput, calls=%fused_computation.3 | convolution fusion | flops 2155872256 | bytes 11534336 | tf_op jit(solution)/shard_map/tf,td->fd/dot_general | solution.py:60
  123.0 6.3 %collective-permute-start.3 = (bf16[1024,2048]{1,0:T(8,128)(2,1)S(1)}, bf16[1024,2048]{1,0:T(8,128)(2,1)S(1)}, u32[]{:S(2)}, u32[]{:S(2)}) collective-permute-start(bf16[1024,2048]{1,0:T(8,128)(2,1)S(1)} %subtract_convert_fusion), channel_id=1, source_target_pairs={{0,124},{4,0},{8,4},{12,8},{16,12},{20,16},{24,20},{28,24},{32,28}... | collective-permute-start | bytes 12582920 | tf_op jit(solution)/shard_map/ppermute | solution.py:12
  129.3 259.2 %collective-permute-done.3 = bf16[1024,2048]{1,0:T(8,128)(2,1)S(1)} collective-permute-done((bf16[1024,2048]{1,0:T(8,128)(2,1)S(1)}, bf16[1024,2048]{1,0:T(8,128)(2,1)S(1)}, u32[]{:S(2)}, u32[]{:S(2)}) %collective-permute-start.3) | collective-permute-done | bytes 4194336 | tf_op jit(solution)/shard_map/ppermute | solution.py:12
  388.5 2.0 copy-done.3
  390.5 4.5 %collective-permute-done.2 = bf16[1024,2048]{1,0:T(8,128)(2,1)} collective-permute-done((bf16[1024,2048]{1,0:T(8,128)(2,1)S(1)}, bf16[1024,2048]{1,0:T(8,128)(2,1)}, u32[]{:S(2)}, u32[]{:S(2)}) %collective-permute-start.2) | collective-permute-done | bytes 4194336 | tf_op jit(solution)/shard_map/ppermute | solution.py:12
  395.0 10.1 %fusion.1 = bf16[1,1024,2048]{2,1,0:T(8,128)(2,1)} fusion(bf16[1024,2048]{1,0:T(8,128)(2,1)} %copy-done.3, bf16[1024,2048]{1,0:T(8,128)(2,1)} %copy-done.2, bf16[1024,2048]{1,0:T(8,128)(2,1)} %collective-permute-done.2), kind=kLoop, calls=%fused_computation.9 | loop fusion | flops 14680064 | bytes 16777216 | tf_op jit(solution)/shard_map/broadcast_in_dim | solution.py:90
  405.1 9.2 %multiply_convert_fusion = bf16[2,2048,1024]{2,1,0:T(8,128)(2,1)S(1)} fusion(bf16[2,2048,1024]{2,1,0:T(8,128)(2,1)} %collective-permute-done.1, bf16[2,2048,1024]{2,1,0:T(8,128)(2,1)} %collective-permute-done, bf16[1,2048,1024]{2,1,0:T(8,128)(2,1)S(1)} %fusion.11, bf16[1,2048,1024]{2,1,0:T(8,128)(2,1)S(1)} %copy-done), kind=kLoop, calls=%fused_computation | loop fusion | flops 33554432 | bytes 33554432 | tf_op jit(solution)/shard_map/convert_element_type | solution.py:24
  414.3 3.8 fusion.33
  (31 shorter events, 0.1 us)
Async XLA Ops:
  7.2 57.1 %reduce-scatter.2.cloned.1.call-start = ((), (), s32[]{:S(2)}) async-start(), calls=%async_computation.1 | async-start | bytes 2621440 | tf_op jit(solution)/shard_map/reduce_scatter | solution.py:52
  9.3 5.4 %copy-start.1 = (bf16[1,512,2048]{2,1,0:T(8,128)(2,1)S(1)}, bf16[1,512,2048]{2,1,0:T(8,128)(2,1)}, u32[]{:S(2)}) copy-start(bf16[1,512,2048]{2,1,0:T(8,128)(2,1)} %param.5) | copy-start | bytes 6291460
  9.3 5.4 %copy-start.4 = (bf16[1,2048,1024]{2,1,0:T(8,128)(2,1)S(1)}, bf16[1,2048,1024]{2,1,0:T(8,128)(2,1)}, u32[]{:S(2)}) copy-start(bf16[1,2048,1024]{2,1,0:T(8,128)(2,1)} %param.8) | copy-start | bytes 12582916
  14.7 4.0 copy-start.9
  14.7 5.0 %copy-start.7 = (bf16[1,1024,2048]{2,1,0:T(8,128)(2,1)S(1)}, bf16[1,1024,2048]{2,1,0:T(8,128)(2,1)}, u32[]{:S(2)}) copy-start(bf16[1,1024,2048]{2,1,0:T(8,128)(2,1)} %param.9) | copy-start | bytes 12582916
  18.7 1.0 copy-start.11
  23.4 69.7 %all-gather.2.cloned.1.call-start = ((), (), s32[]{:S(2)}) async-start(), calls=%async_computation.2 | async-start | bytes 2621440 | tf_op jit(solution)/shard_map/all_gather | solution.py:58
  93.1 5.3 %copy-start.5 = (bf16[1,2048,1024]{2,1,0:T(8,128)(2,1)S(1)}, bf16[1,2048,1024]{2,1,0:T(8,128)(2,1)}, u32[]{:S(2)}) copy-start(bf16[1,2048,1024]{2,1,0:T(8,128)(2,1)} %param.8) | copy-start | bytes 12582916
  93.1 5.4 %copy-start.10 = (f32[512,1024]{1,0:T(8,128)S(1)}, f32[512,1024]{1,0:T(8,128)}, u32[]{:S(2)}) copy-start(f32[512,1024]{1,0:T(8,128)} %copy-done.9) | copy-start | bytes 6291460
  98.5 3.1 copy-start.6
  98.5 3.1 copy-start.12
  106.4 11.4 %copy-start.8 = (bf16[512,2048]{1,0:T(8,128)(2,1)S(1)}, bf16[512,2048]{1,0:T(8,128)(2,1)}, u32[]{:S(2)}) copy-start(bf16[512,2048]{1,0:T(8,128)(2,1)} %all-gather.2.cloned.1.call-done) | copy-start | bytes 6291460
  112.8 292.4 %collective-permute-start.1 = (bf16[2,2048,1024]{2,1,0:T(8,128)(2,1)}, bf16[2,2048,1024]{2,1,0:T(8,128)(2,1)}, u32[]{:S(2)}, u32[]{:S(2)}) collective-permute-start(bf16[2,2048,1024]{2,1,0:T(8,128)(2,1)} %pad_maximum_fusion), channel_id=1, source_target_pairs={{0,124},{4,0},{8,4},{12,8},{16,12},{20,16},{24,20},{28,24},{32,28}... | collective-permute-start | bytes 25165832 | tf_op jit(solution)/shard_map/ppermute | solution.py:12
  117.9 287.3 %collective-permute-start = (bf16[2,2048,1024]{2,1,0:T(8,128)(2,1)}, bf16[2,2048,1024]{2,1,0:T(8,128)(2,1)}, u32[]{:S(2)}, u32[]{:S(2)}) collective-permute-start(bf16[2,2048,1024]{2,1,0:T(8,128)(2,1)} %pad_maximum_fusion), channel_id=1, source_target_pairs={{0,4},{4,8},{8,12},{12,16},{16,20},{20,24},{24,28},{28,32},{32,36}... | collective-permute-start | bytes 25165832 | tf_op jit(solution)/shard_map/ppermute | solution.py:12
  122.9 6.3 %copy-start.2 = (bf16[1024,2048]{1,0:T(8,128)(2,1)}, bf16[1024,2048]{1,0:T(8,128)(2,1)S(1)}, u32[]{:S(2)}) copy-start(bf16[1024,2048]{1,0:T(8,128)(2,1)S(1)} %subtract_convert_fusion) | copy-start | bytes 12582916
  122.9 282.2 %copy-start = (bf16[1,2048,1024]{2,1,0:T(8,128)(2,1)S(1)}, bf16[1,2048,1024]{2,1,0:T(8,128)(2,1)}, u32[]{:S(2)}) copy-start(bf16[1,2048,1024]{2,1,0:T(8,128)(2,1)} %fusion.10) | copy-start | bytes 12582916
  123.0 265.6 %collective-permute-start.3 = (bf16[1024,2048]{1,0:T(8,128)(2,1)S(1)}, bf16[1024,2048]{1,0:T(8,128)(2,1)S(1)}, u32[]{:S(2)}, u32[]{:S(2)}) collective-permute-start(bf16[1024,2048]{1,0:T(8,128)(2,1)S(1)} %subtract_convert_fusion), channel_id=1, source_target_pairs={{0,124},{4,0},{8,4},{12,8},{16,12},{20,16},{24,20},{28,24},{32,28}... | collective-permute-start | bytes 12582920 | tf_op jit(solution)/shard_map/ppermute | solution.py:12
  129.3 265.8 %collective-permute-start.2 = (bf16[1024,2048]{1,0:T(8,128)(2,1)S(1)}, bf16[1024,2048]{1,0:T(8,128)(2,1)}, u32[]{:S(2)}, u32[]{:S(2)}) collective-permute-start(bf16[1024,2048]{1,0:T(8,128)(2,1)S(1)} %subtract_convert_fusion), channel_id=1, source_target_pairs={{0,4},{4,8},{8,12},{12,16},{16,20},{20,24},{24,28},{28,32},{32,36}... | collective-permute-start | bytes 12582920 | tf_op jit(solution)/shard_map/ppermute | solution.py:12
  388.5 2.0 copy-start.3
Sparse Core Ops, SparseCore 0:
  23.5 40.6 reduce-scatter.1
  66.9 26.1 all-gather.1
where the time goes:
time: 425 us
  waiting for transfers between devices  328 us (77%)
  other arithmetic  32.8 us (8%)
  matrix products  31.3 us (7%)
  between operations  14.2 us (3%)
  starting transfers between devices  11.7 us (3%)
  local copies, waits for them, and re-layouts  6.84 us (2%)
    ppermute x4, waiting for transfers between devices, passed_along(): return lax.ppermute(value, axis, pairs)  264 us
    reduce_scatter x1, waiting for transfers between devices, local(): lax.psum_scatter(partial_value.astype(jnp.bfloat16), 'mp', scatter_dimens...  38.1 us
    all_gather x1, waiting for transfers between devices, local(): err_grad = lax.all_gather(err_own, 'mp', axis=0, tiled=True)  26.3 us
    ppermute x4, starting transfers between devices, passed_along(): return lax.ppermute(value, axis, pairs)  11.4 us
    broadcast_in_dim x1, other arithmetic, local(): return (w_gate[None], w_up[None], w_down[None])  10.1 us
    convert_element_type x1, other arithmetic, mix_three(): return (total / 3.0).astype(jnp.bfloat16)  9.17 us
  transfers between devices with their start and end apart: 6, of which 4 were waited for; matrix products, arithmetic and copies ran while one was open for 4% of the time, Pallas kernels for 0%

commit v1 on v0

v1 whole, which is shorter than its diff:
```python
import jax
import jax.numpy as jnp
from jax import lax
from jax.experimental import pallas as pl
from jax.experimental.pallas import tpu as pltpu
from jax.sharding import PartitionSpec as P


SIZES = (256, 256, 512)
UP_ROWS = (1536, 256, 128, 128)
BLOCK = 256
MIB = 1024 * 1024


def along_cycle(value, steps):
    count = lax.axis_size("gossip")
    return lax.ppermute(value, "gossip", [(s, (s + steps) % count) for s in range(count)])


def other_core(value):
    count = lax.axis_size("mp")
    return lax.ppermute(value, "mp", [(s, s ^ 1) for s in range(count)])


def other_chip(value):
    count = lax.axis_size("mp")
    return lax.ppermute(value, "mp", [(s, s ^ 2) for s in range(count)])


def both_ways(value):
    lower = along_cycle(value, 1)
    upper = along_cycle(value, -1)
    return lower, value, upper


def mix_three(lower, own, upper):
    total = lower.astype(jnp.float32) + own.astype(jnp.float32) + upper.astype(jnp.float32)
    return (total / 3.0).astype(jnp.bfloat16)


def mix_rows(before, rows_out, start, parts):
    rows, width = parts[1].shape
    block = min(rows, 256)

    def body(lower, own, upper, *rest):
        rest[-1][...] = mix_three(lower[...], own[...], upper[...])

    piece = pl.BlockSpec((block, width), lambda n: (n, 0))
    aliased = before is not None and before.shape[0] == rows_out
    extra = [] if before is None else [before]
    return pl.pallas_call(
        body,
        grid=(rows // block,),
        in_specs=[piece] * 3 + [pl.BlockSpec(memory_space=pl.ANY)] * len(extra),
        out_specs=pl.BlockSpec((block, width), lambda n: (start // block + n, 0)),
        out_shape=jax.ShapeDtypeStruct((rows_out, width), jnp.bfloat16),
        input_output_aliases={3: 0} if start else {},
        compiler_params=pltpu.CompilerParams(vmem_limit_bytes=56 * MIB),
    )(*parts, *extra)


def dot(a, b, dims):
    return lax.dot_general(a, b, (dims, ((), ())), preferred_element_type=jnp.float32)


def forward_body(core, *refs, in_scale):
    count = len(SIZES)
    tokens, targets, w_gate, w_up, w_down = refs[:5]
    outs = refs[5 : 9 + 3 * count]
    (
        tok, gate_v, up_v, down_t, down_m, wanted,
        hidden, hidden_t, slope, act, normed, theirs, mine, offset, in_sems, out_sems,
    ) = refs[9 + 3 * count :]
    rows, width = tok.shape
    half = width // 2
    blocks = hidden.shape[1] // BLOCK
    at_mine = pl.multiple_of(core[0] * half, half)
    at_theirs = pl.multiple_of((1 - core[0]) * half, half)

    def fetch(n, src, dst):
        return pltpu.make_async_copy(src, dst, in_sems.at[n])

    def put(n, src, dst):
        copy = pltpu.make_async_copy(src, dst, out_sems.at[n])
        copy.start()
        return copy

    def span(n):
        return slice(n * BLOCK, (n + 1) * BLOCK)

    tok_copies = [
        fetch(n, tokens.at[part], tok.at[part])
        for n, part in enumerate((slice(0, rows // 2), slice(rows // 2, rows)))
    ]
    weight_copies = [
        (
            fetch(2 + 2 * n, w_gate.at[:, span(n)], gate_v.at[:, span(n)]),
            fetch(3 + 2 * n, w_up.at[:, span(n)], up_v.at[:, span(n)]),
        )
        for n in range(blocks)
    ]
    base = 2 + 2 * blocks
    copy_t = fetch(base, w_down.at[:, pl.ds(at_theirs, half)], down_t)
    copy_m = fetch(base + 1, w_down.at[:, pl.ds(at_mine, half)], down_m)
    copy_w = fetch(base + 2, targets.at[:, pl.ds(at_mine, half)], wanted)

    for copy in (*tok_copies, *weight_copies[0]):
        copy.start()
    for n, copy in enumerate(tok_copies):
        copy.wait()
        part = slice(n * (rows // 2), (n + 1) * (rows // 2))
        wide = tok[part].astype(jnp.float32)
        scale = lax.rsqrt(jnp.mean(wide * wide, axis=-1, keepdims=True) + 1e-06)
        normed[part] = (wide * scale).astype(jnp.bfloat16)
        if n == 0:
            for copy in weight_copies[1]:
                copy.start()
    done = [put(0, normed, outs[3])]
    later = [weight_copies[2], weight_copies[3], (copy_t, copy_w), (copy_m,)]
    for n in range(blocks):
        for copy in later[n]:
            copy.start()
        for copy in weight_copies[n]:
            copy.wait()
        cols = span(n)
        gate_pre = jnp.dot(normed[...], gate_v[:, cols], preferred_element_type=jnp.float32)
        up_pre = jnp.dot(normed[...], up_v[:, cols], preferred_element_type=jnp.float32)
        gate_pre = gate_pre * in_scale
        up_pre = up_pre * in_scale
        sig = jax.nn.sigmoid(gate_pre)
        activated = gate_pre * sig
        value = (activated * up_pre).astype(jnp.bfloat16)
        hidden[:, cols] = value
        hidden_t[cols] = value.T
        act[:, cols] = activated
        slope[:, cols] = up_pre * (sig * (1.0 + gate_pre * (1.0 - sig)))
        done.append(put(1 + 3 * n, hidden_t.at[cols], outs[0].at[cols]))
        done.append(put(2 + 3 * n, slope.at[:, cols], outs[1].at[:, cols]))
        done.append(put(3 + 3 * n, act.at[:, cols], outs[2].at[:, cols]))
    at_sem = 1 + 3 * blocks
    copy_w.wait()
    copy_t.wait()
    at = 0
    for n, size in enumerate(SIZES):
        cols = slice(at, at + size)
        theirs[:, cols] = jnp.dot(
            hidden[...], down_t[:, cols], preferred_element_type=jnp.float32
        ).astype(jnp.bfloat16)
        done.append(put(at_sem + 3 * n, theirs.at[:, cols], outs[4 + n]))
        at += size
    copy_m.wait()
    at = 0
    for n, size in enumerate(SIZES):
        cols = slice(at, at + size)
        at_tok = pl.multiple_of(core[0] * half + at, 128)
        offset[:, cols] = tok[:, pl.ds(at_tok, size)].astype(jnp.float32) - wanted[:, cols].astype(
            jnp.float32
        )
        done.append(put(at_sem + 3 * n + 2, offset.at[:, cols], outs[4 + 2 * count + n]))
        mine[:, cols] = jnp.dot(hidden[...], down_m[:, cols], preferred_element_type=jnp.float32)
        done.append(put(at_sem + 3 * n + 1, mine.at[:, cols], outs[4 + count + n]))
        at += size
    for copy in done:
        copy.wait()


def forward(core, tokens, targets, w_gate, w_up, w_down, in_scale):
    rows, width = tokens.shape
    count = w_gate.shape[1]
    half = width // 2
    anywhere = pl.BlockSpec(memory_space=pl.ANY)
    narrow = [jax.ShapeDtypeStruct((rows, size), jnp.bfloat16) for size in SIZES]
    wide = [jax.ShapeDtypeStruct((rows, size), jnp.float32) for size in SIZES]
    outs = [
        jax.ShapeDtypeStruct((count, rows), jnp.bfloat16),
        jax.ShapeDtypeStruct((rows, count), jnp.float32),
        jax.ShapeDtypeStruct((rows, count), jnp.float32),
        jax.ShapeDtypeStruct((rows, width), jnp.bfloat16),
        *narrow,
        *wide,
        *wide,
    ]
    blocks = count // BLOCK
    return pl.pallas_call(
        lambda *refs: forward_body(*refs, in_scale=in_scale),
        name="forward",
        in_specs=[pl.BlockSpec(memory_space=pltpu.SMEM)] + [anywhere] * 5,
        out_specs=[anywhere] * len(outs),
        out_shape=outs,
        scratch_shapes=[
            pltpu.VMEM((rows, width), jnp.bfloat16),
            pltpu.VMEM((width, count), jnp.bfloat16),
            pltpu.VMEM((width, count), jnp.bfloat16),
            pltpu.VMEM((count, half), jnp.bfloat16),
            pltpu.VMEM((count, half), jnp.bfloat16),
            pltpu.VMEM((rows, half), jnp.bfloat16),
            pltpu.VMEM((rows, count), jnp.bfloat16),
            pltpu.VMEM((count, rows), jnp.bfloat16),
            pltpu.VMEM((rows, count), jnp.float32),
            pltpu.VMEM((rows, count), jnp.float32),
            pltpu.VMEM((rows, width), jnp.bfloat16),
            pltpu.VMEM((rows, half), jnp.bfloat16),
            pltpu.VMEM((rows, half), jnp.float32),
            pltpu.VMEM((rows, half), jnp.float32),
            pltpu.SemaphoreType.DMA((2 + 2 * blocks + 3,)),
            pltpu.SemaphoreType.DMA((1 + 3 * blocks + 3 * len(SIZES),)),
        ],
        compiler_params=pltpu.CompilerParams(vmem_limit_bytes=58 * MIB),
    )(core[None].astype(jnp.int32), tokens, targets, w_gate, w_up, w_down)


def compute(tokens, targets, gate_weight, up_weight, down_weight):
    inputs = tokens[0]
    wanted = targets[0]
    w_gate = gate_weight[0]
    w_up = up_weight[0]
    w_down = down_weight[0]
    tok_count, width = inputs.shape
    mp_count = lax.axis_size("mp")
    hidden_all = w_gate.shape[1] * mp_count
    in_scale = 1.0 / width**0.5
    mid_scale = 1.0 / hidden_all**0.5
    step_size = hidden_all / 4.0
    half = width // 2
    core = lax.axis_index("mp") % 2
    mine = core * half
    theirs = half - mine

    outs = forward(core, inputs, wanted, w_gate, w_up, w_down, in_scale)
    hidden_t, slope_gate, act, normed = outs[:4]
    count = len(SIZES)
    sums_theirs, sums_mine, offsets = (outs[4 + n * count : 4 + (n + 1) * count] for n in range(3))

    def columns(array, start, size):
        return lax.dynamic_slice_in_dim(array, start, size, 1)

    def stepped_down(err, start):
        grad = dot(hidden_t, err, ((1,), (0,))) * mid_scale
        w_piece = columns(w_down, start, err.shape[1])
        new = (w_piece.astype(jnp.float32) - step_size * grad).astype(jnp.bfloat16)
        down_parts.append((start, both_ways(new)))

    totals = []
    far = []
    for n in range(count):
        arrived = other_core(sums_theirs[n])
        total = sums_mine[n] + arrived.astype(jnp.float32)
        rounded = total.astype(jnp.bfloat16)
        totals.append(total)
        far.append(other_chip(rounded))

    err_mine = []
    err_theirs = []
    down_parts = []
    at = 0
    for n, size in enumerate(SIZES):
        output = (totals[n] + far[n].astype(jnp.float32)) * mid_scale
        err = ((offsets[n] + output) / tok_count).astype(jnp.bfloat16)
        err_mine.append(err)
        err_theirs.append(other_core(err))
        stepped_down(err, mine + at)
        at += size
        if n == 1:
            first = jnp.concatenate(err_theirs, 1)
            stepped_down(first, theirs)
    stepped_down(err_theirs[2], theirs + SIZES[0] + SIZES[1])

    err_m = jnp.concatenate(err_mine, 1)
    err_t = jnp.concatenate([first, err_theirs[2]], 1)
    grad_hidden = (
        dot(err_m, columns(w_down, mine, half), ((1,), (1,)))
        + dot(err_t, columns(w_down, theirs, half), ((1,), (1,)))
    ) * mid_scale
    grad_gate = (grad_hidden * slope_gate).astype(jnp.bfloat16)
    grad_up = (grad_hidden * act).astype(jnp.bfloat16)

    def stepped(weight, grad_in, row, rows):
        grad_w = dot(normed[:, row : row + rows], grad_in, ((0,), (0,))) * in_scale
        new = (weight[row : row + rows].astype(jnp.float32) - step_size * grad_w).astype(
            jnp.bfloat16
        )
        return both_ways(new)

    gate_parts = stepped(w_gate, grad_gate, 0, width)
    up_parts = []
    row = 0
    for rows in UP_ROWS:
        up_parts.append((row, stepped(w_up, grad_up, row, rows)))
        row += rows

    down_out = jnp.zeros_like(w_down)
    for start, parts in down_parts:
        down_out = lax.dynamic_update_slice(down_out, mix_three(*parts), (0, start))
    gate_out = mix_rows(None, width, 0, gate_parts)
    up_out = gate_out[:16]
    for start, parts in up_parts:
        up_out = mix_rows(up_out, width, start, parts)
    return gate_out[None], up_out[None], down_out[None]


def solution(mesh):
    placed = (
        P("gossip", None, None),
        P("gossip", None, None),
        P("gossip", None, "mp"),
        P("gossip", None, "mp"),
        P("gossip", "mp", None),
    )
    return jax.shard_map(
        compute,
        mesh=mesh,
        in_specs=placed,
        out_specs=(P("gossip", None, "mp"), P("gossip", None, "mp"), P("gossip", "mp", None)),
        check_vma=False,
    )
```

time: 425 us -> 400 us (0.941)
  waiting for transfers between devices: 328 us -> 269 us
  starting transfers between devices: 11.7 us -> 56.8 us
  Pallas kernels: 0 us -> 35.7 us
  other arithmetic: 32.8 us -> 7.57 us
  between operations: 14.2 us -> 1.19 us
  matrix products: 31.3 us -> 21.1 us
    ppermute x4 -> x29, starting transfers between devices: 11.4 us -> 56.8 us  [the longest x20 49.3 us: along_cycle(): lax.ppermute(value, 'gossip', [(s, (s + steps) % count) for s in range(co...]
    reduce_scatter x1 -> x0, waiting for transfers between devices: 38.1 us -> none  [local(): lax.psum_scatter(partial_value.astype(jnp.bfloat16), 'mp', scatter_dimens...]
    pallas_call x0 -> x6, Pallas kernels: none -> 35.7 us  [the longest x5 23.2 us: mix_rows(): pl.pallas_call(body, grid=(rows // block,), in_specs=[piece] * 3 + [pl.Bl...]
    all_gather x1 -> x0, waiting for transfers between devices: 26.3 us -> none  [local(): err_grad = lax.all_gather(err_own, 'mp', axis=0, tiled=True)]
    convert_element_type x3 -> x6, other arithmetic: 14.2 us -> 3.16 us  [the longest x3 2.48 us: compute(): rounded = total.astype(jnp.bfloat16)]
    dot_general x7 -> x12, matrix products: 31.3 us -> 21.1 us  [dot(): lax.dot_general(a, b, (dims, ((), ())), preferred_element_type=jnp.float32)]
    broadcast_in_dim x1 -> x0, other arithmetic: 10.1 us -> none  [local(): return (w_gate[None], w_up[None], w_down[None])]
    another operation x1 -> x0, other arithmetic: 6.34 us -> none  [local(): inner = jnp.stack([new_gate, new_up])]
  transfers between devices with their start and end apart: 6 -> 29, of which waited for: 4 -> 8; matrix products, arithmetic and copies ran while one was open for 4% -> 8% of each run, Pallas kernels for 0% -> 5%
where the time goes in v1:
time: 400 us; the launch traced here: 399 us
  waiting for transfers between devices  269 us (67%)
  starting transfers between devices  56.8 us (14%)
  Pallas kernels  35.7 us (9%)
  matrix products  21.1 us (5%)
  local copies, waits for them, and re-layouts  7.98 us (2%)
  other arithmetic  7.57 us (2%)
    ppermute x20, waiting for transfers between devices, along_cycle(): lax.ppermute(value, 'gossip', [(s, (s + steps) % count) for s in range(co...  240 us
    ppermute x20, starting transfers between devices, along_cycle(): lax.ppermute(value, 'gossip', [(s, (s + steps) % count) for s in range(co...  49.3 us
    ppermute x3, waiting for transfers between devices, other_chip(): return lax.ppermute(value, 'mp', [(s, s ^ 2) for s in range(count)])  27.4 us
    pallas_call x5, Pallas kernels, mix_rows(): pl.pallas_call(body, grid=(rows // block,), in_specs=[piece] * 3 + [pl.Bl...  23.2 us
    dot_general x12, matrix products, dot(): lax.dot_general(a, b, (dims, ((), ())), preferred_element_type=jnp.float32)  21.1 us
    pallas_call x1, Pallas kernels, forward(): pl.pallas_call(lambda *refs: forward_body(*refs, in_scale=in_scale), name...  12.5 us
  transfers between devices with their start and end apart: 29, of which 8 were waited for; matrix products, arithmetic and copies ran while one was open for 8% of the time, Pallas kernels for 5%

profile of v1, /device:TPU:0, one launch (start us, length us, event | category | flops | bytes accessed | tf_op | source)
XLA Modules:
  0.0 399.3 jit_solution(14615638244927155622)
XLA Ops:
  0.6 12.5 %forward.1 = (bf16[1024,512]{1,0:T(8,128)(2,1)}, f32[512,1024]{1,0:T(8,128)}, f32[512,1024]{1,0:T(8,128)}, bf16[512,2048]{1,0:T(8,128)(2,1)}, bf16[512,256]{1,0:...) custom-call(s32[1]{0:T(128)} %bitcast.1.refs_0_, ...), custom_call_target="tpu_custom_call" | custom-call | tf_op jit(solution)/shard_map/forward/pallas_call | solution.py:184
  16.1 3.4 collective-permute-start.1
  21.0 5.8 %collective-permute-done.1 = bf16[512,256]{1,0:T(8,128)(2,1)S(1)} collective-permute-done((bf16[512,256]{1,0:T(8,128)(2,1)S(1)}, bf16[512,256]{1,0:T(8,128)(2,1)S(1)}, u32[]{:S(2)}, u32[]{:S(2)}) %collective-permute-start.1) | collective-permute-done | bytes 262176 | tf_op jit(solution)/shard_map/ppermute | solution.py:27
  28.8 7.5 %collective-permute-start.20 = (bf16[1024,256]{1,0:T(8,128)(2,1)S(1)}, bf16[1024,256]{1,0:T(8,128)(2,1)S(1)}, u32[]{:S(2)}, u32[]{:S(2)}) collective-permute-start(bf16[1024,256]{1,0:T(8,128)(2,1)S(1)} %fusion.17), channel_id=1, source_target_pairs={{0,124},{4,0},{8,4},{12,8},{16,12},{20,16},{24,20},{28,24},{32,28}... | collective-permute-start | bytes 1572872 | tf_op jit(solution)/shard_map/ppermute | solution.py:17
  36.4 3.0 collective-permute-start.5
  40.2 21.6 %collective-permute-done.5 = bf16[512,512]{1,0:T(8,128)(2,1)S(1)} collective-permute-done((bf16[512,512]{1,0:T(8,128)(2,1)S(1)}, bf16[512,512]{1,0:T(8,128)(2,1)S(1)}, u32[]{:S(2)}, u32[]{:S(2)}) %collective-permute-start.5) | collective-permute-done | bytes 524320 | tf_op jit(solution)/shard_map/ppermute | solution.py:27
  61.7 3.1 collective-permute-start.22
  68.3 6.2 %collective-permute-start.24 = (bf16[1024,512]{1,0:T(8,128)(2,1)S(1)}, bf16[1024,512]{1,0:T(8,128)(2,1)S(1)}, u32[]{:S(2)}, u32[]{:S(2)}) collective-permute-start(bf16[1024,512]{1,0:T(8,128)(2,1)S(1)} %fusion.3), channel_id=1, source_target_pairs={{0,124},{4,0},{8,4},{12,8},{16,12},{20,16},{24,20},{28,24},{32,28}... | collective-permute-start | bytes 3145736 | tf_op jit(solution)/shard_map/ppermute | solution.py:17
  75.9 6.2 %collective-permute-start.26 = (bf16[1024,512]{1,0:T(8,128)(2,1)S(1)}, bf16[1024,512]{1,0:T(8,128)(2,1)S(1)}, u32[]{:S(2)}, u32[]{:S(2)}) collective-permute-start(bf16[1024,512]{1,0:T(8,128)(2,1)S(1)} %fusion.2), channel_id=1, source_target_pairs={{0,124},{4,0},{8,4},{12,8},{16,12},{20,16},{24,20},{28,24},{32,28}... | collective-permute-start | bytes 3145736 | tf_op jit(solution)/shard_map/ppermute | solution.py:17
  82.2 4.7 %subtract_convert_fusion.own = bf16[2048,1024]{1,0:T(8,128)(2,1)} fusion(bf16[512,2048]{1,0:T(8,128)(2,1)S(1)} %copy-done.37, f32[512,1024]{1,0:T(8,128)S(1)} %get-tuple-element.30, f32[512,1024]{1,0:T(8,128)S(1)} %copy-done.38, bf16[1,2048,1024]{2,1,0:T(8,128)(2,1)S(1)} %copy-done.2), kind=kOutput, calls=%fused_computation | convolution fusion | flops 2156920832 | bytes 14680064 | tf_op jit(solution)/shard_map/dot_general | solution.py:63
  86.9 6.2 %collective-permute-start.10 = (bf16[2048,1024]{1,0:T(8,128)(2,1)}, bf16[2048,1024]{1,0:T(8,128)(2,1)}, u32[]{:S(2)}, u32[]{:S(2)}) collective-permute-start(bf16[2048,1024]{1,0:T(8,128)(2,1)} %subtract_convert_fusion.own), channel_id=1, source_target_pairs={{0,124},{4,0},{8,4},{12,8},{16,12},{20,16},{24,20},{28,24},{32,28}... | collective-permute-start | bytes 12582920 | tf_op jit(solution)/shard_map/ppermute | solution.py:17
  93.7 6.0 %collective-permute-done.24 = bf16[1024,512]{1,0:T(8,128)(2,1)S(1)} collective-permute-done((bf16[1024,512]{1,0:T(8,128)(2,1)S(1)}, bf16[1024,512]{1,0:T(8,128)(2,1)S(1)}, u32[]{:S(2)}, u32[]{:S(2)}) %collective-permute-start.24) | collective-permute-done | bytes 1048608 | tf_op jit(solution)/shard_map/ppermute | solution.py:17
  99.7 6.5 %collective-permute-done.23 = bf16[1024,512]{1,0:T(8,128)(2,1)S(1)} collective-permute-done((bf16[1024,512]{1,0:T(8,128)(2,1)S(1)}, bf16[1024,512]{1,0:T(8,128)(2,1)S(1)}, u32[]{:S(2)}, u32[]{:S(2)}) %collective-permute-start.23) | collective-permute-done | bytes 1048608 | tf_op jit(solution)/shard_map/ppermute | solution.py:17
  106.1 3.7 fusion.own
  109.9 119.4 %collective-permute-done.15.lower = bf16[256,1024]{1,0:T(8,128)(2,1)S(1)} collective-permute-done((bf16[256,1024]{1,0:T(8,128)(2,1)S(1)}, bf16[256,1024]{1,0:T(8,128)(2,1)S(1)}, u32[]{:S(2)}, u32[]{:S(2)}) %collective-permute-start.15) | collective-permute-done | bytes 524320 | tf_op jit(solution)/shard_map/ppermute | solution.py:17
  231.0 5.5 %collective-permute-start.18 = (bf16[1536,1024]{1,0:T(8,128)(2,1)}, bf16[1536,1024]{1,0:T(8,128)(2,1)}, u32[]{:S(2)}, u32[]{:S(2)}) collective-permute-start(bf16[1536,1024]{1,0:T(8,128)(2,1)} %fusion.own), channel_id=1, source_target_pairs={{0,124},{4,0},{8,4},{12,8},{16,12},{20,16},{24,20},{28,24},{32,28}... | collective-permute-start | bytes 9437192 | tf_op jit(solution)/shard_map/ppermute | solution.py:17
  236.5 2.4 fusion.1
  241.5 84.5 %collective-permute-done.28 = bf16[1024,512]{1,0:T(8,128)(2,1)S(1)} collective-permute-done((bf16[1024,512]{1,0:T(8,128)(2,1)S(1)}, bf16[1024,512]{1,0:T(8,128)(2,1)S(1)}, u32[]{:S(2)}, u32[]{:S(2)}) %collective-permute-start.28) | collective-permute-done | bytes 1048608 | tf_op jit(solution)/shard_map/ppermute | solution.py:17
  330.5 24.0 %collective-permute-done.27 = bf16[1024,512]{1,0:T(8,128)(2,1)S(1)} collective-permute-done((bf16[1024,512]{1,0:T(8,128)(2,1)S(1)}, bf16[1024,512]{1,0:T(8,128)(2,1)S(1)}, u32[]{:S(2)}, u32[]{:S(2)}) %collective-permute-start.27) | collective-permute-done | bytes 1048608 | tf_op jit(solution)/shard_map/ppermute | solution.py:17
  358.3 6.0 %collective-permute-start.12 = (bf16[128,1024]{1,0:T(8,128)(2,1)S(1)}, bf16[128,1024]{1,0:T(8,128)(2,1)S(1)}, u32[]{:S(2)}, u32[]{:S(2)}) collective-permute-start(bf16[128,1024]{1,0:T(8,128)(2,1)S(1)} %fusion.22.own), channel_id=1, source_target_pairs={{0,124},{4,0},{8,4},{12,8},{16,12},{20,16},{24,20},{28,24},{32,28}... | collective-permute-start | bytes 786440 | tf_op jit(solution)/shard_map/ppermute | solution.py:17
  364.3 6.2 %collective-permute-start.14 = (bf16[128,1024]{1,0:T(8,128)(2,1)}, bf16[128,1024]{1,0:T(8,128)(2,1)S(1)}, u32[]{:S(2)}, u32[]{:S(2)}) collective-permute-start(bf16[128,1024]{1,0:T(8,128)(2,1)} %fusion.21.own), channel_id=1, source_target_pairs={{0,124},{4,0},{8,4},{12,8},{16,12},{20,16},{24,20},{28,24},{32,28}... | collective-permute-start | bytes 786440 | tf_op jit(solution)/shard_map/ppermute | solution.py:17
  371.1 10.1 %shard_map.76 = bf16[2048,1024]{1,0:T(8,128)(2,1)} custom-call(bf16[2048,1024]{1,0:T(8,128)(2,1)} %collective-permute-done.9.lower, bf16[2048,1024]{1,0:T(8,128)(2,1)} %subtract_convert_fusion.own, bf16[2048,1024]{1,0:T(8,128)(2,1)} %collective-permute-done.10.upper), custom_call_target="tpu_custom_call" | custom-call | tf_op jit(solution)/shard_map/pallas_call | solution.py:51
  382.5 6.9 %shard_map.77.rest_0_ = bf16[2048,1024]{1,0:T(8,128)(2,1)} custom-call(bf16[1536,1024]{1,0:T(8,128)(2,1)} %collective-permute-done.17.lower, bf16[1536,1024]{1,0:T(8,128)(2,1)} %fusion.own, bf16[1536,1024]{1,0:T(8,128)(2,1)} %collective-permute-done.18.upper, bf16[16,1024]{1,0:T(8,128)(2,1)} %slice.40.rest_0_), custom_call_target="tpu_custom_call" | custom-call | tf_op jit(solution)/shard_map/pallas_call | solution.py:51
  390.2 2.4 shard_map.78.rest_0_
  (145 shorter events, 34.4 us)
Async XLA Ops:
  20.7 18.7 %collective-permute-start.3 = (bf16[512,256]{1,0:T(8,128)(2,1)S(1)}, bf16[512,256]{1,0:T(8,128)(2,1)S(1)}, u32[]{:S(2)}, u32[]{:S(2)}) collective-permute-start(bf16[512,256]{1,0:T(8,128)(2,1)S(1)} %fusion.48), channel_id=1, source_target_pairs={{0,2},{1,3},{2,0},{3,1},{4,6},{5,7},{6,4},{7,5},{8,10},{9,11},{10,... | collective-permute-start | bytes 786440 | tf_op jit(solution)/shard_map/ppermute | solution.py:27
  27.0 38.4 %collective-permute-start.6 = (bf16[512,256]{1,0:T(8,128)(2,1)S(1)}, bf16[512,256]{1,0:T(8,128)(2,1)S(1)}, u32[]{:S(2)}, u32[]{:S(2)}) collective-permute-start(bf16[512,256]{1,0:T(8,128)(2,1)S(1)} %multiply_convert_fusion.10), channel_id=1, source_target_pairs={{0,1},{1,0},{2,3},{3,2},{4,5},{5,4},{6,7},{7,6},{8,9},{9,8},{10,11... | collective-permute-start | bytes 786440 | tf_op jit(solution)/shard_map/ppermute | solution.py:22
  28.8 47.0 %collective-permute-start.20 = (bf16[1024,256]{1,0:T(8,128)(2,1)S(1)}, bf16[1024,256]{1,0:T(8,128)(2,1)S(1)}, u32[]{:S(2)}, u32[]{:S(2)}) collective-permute-start(bf16[1024,256]{1,0:T(8,128)(2,1)S(1)} %fusion.17), channel_id=1, source_target_pairs={{0,124},{4,0},{8,4},{12,8},{16,12},{20,16},{24,20},{28,24},{32,28}... | collective-permute-start | bytes 1572872 | tf_op jit(solution)/shard_map/ppermute | solution.py:17
  36.2 39.7 %collective-permute-start.19 = (bf16[1024,256]{1,0:T(8,128)(2,1)S(1)}, bf16[1024,256]{1,0:T(8,128)(2,1)}, u32[]{:S(2)}, u32[]{:S(2)}) collective-permute-start(bf16[1024,256]{1,0:T(8,128)(2,1)S(1)} %fusion.17), channel_id=1, source_target_pairs={{0,4},{4,8},{8,12},{12,16},{16,20},{20,24},{24,28},{28,32},{32,36}... | collective-permute-start | bytes 1572872 | tf_op jit(solution)/shard_map/ppermute | solution.py:17
  36.4 25.3 %collective-permute-start.5 = (bf16[512,512]{1,0:T(8,128)(2,1)S(1)}, bf16[512,512]{1,0:T(8,128)(2,1)S(1)}, u32[]{:S(2)}, u32[]{:S(2)}) collective-permute-start(bf16[512,512]{1,0:T(8,128)(2,1)S(1)} %fusion.39), channel_id=1, source_target_pairs={{0,2},{1,3},{2,0},{3,1},{4,6},{5,7},{6,4},{7,5},{8,10},{9,11},{10,... | collective-permute-start | bytes 1572872 | tf_op jit(solution)/shard_map/ppermute | solution.py:27
  39.6 25.7 %collective-permute-start.7 = (bf16[512,256]{1,0:T(8,128)(2,1)S(1)}, bf16[512,256]{1,0:T(8,128)(2,1)S(1)}, u32[]{:S(2)}, u32[]{:S(2)}) collective-permute-start(bf16[512,256]{1,0:T(8,128)(2,1)S(1)} %multiply_convert_fusion.9), channel_id=1, source_target_pairs={{0,1},{1,0},{2,3},{3,2},{4,5},{5,4},{6,7},{7,6},{8,9},{9,8},{10,11... | collective-permute-start | bytes 786440 | tf_op jit(solution)/shard_map/ppermute | solution.py:22
  61.7 25.2 %collective-permute-start.22 = (bf16[1024,256]{1,0:T(8,128)(2,1)S(1)}, bf16[1024,256]{1,0:T(8,128)(2,1)S(1)}, u32[]{:S(2)}, u32[]{:S(2)}) collective-permute-start(bf16[1024,256]{1,0:T(8,128)(2,1)S(1)} %fusion.18), channel_id=1, source_target_pairs={{0,124},{4,0},{8,4},{12,8},{16,12},{20,16},{24,20},{28,24},{32,28}... | collective-permute-start | bytes 1572872 | tf_op jit(solution)/shard_map/ppermute | solution.py:17
  65.3 21.6 %collective-permute-start.21 = (bf16[1024,256]{1,0:T(8,128)(2,1)S(1)}, bf16[1024,256]{1,0:T(8,128)(2,1)S(1)}, u32[]{:S(2)}, u32[]{:S(2)}) collective-permute-start(bf16[1024,256]{1,0:T(8,128)(2,1)S(1)} %fusion.18), channel_id=1, source_target_pairs={{0,4},{4,8},{8,12},{12,16},{16,20},{20,24},{24,28},{28,32},{32,36}... | collective-permute-start | bytes 1572872 | tf_op jit(solution)/shard_map/ppermute | solution.py:17
  68.3 31.4 %collective-permute-start.24 = (bf16[1024,512]{1,0:T(8,128)(2,1)S(1)}, bf16[1024,512]{1,0:T(8,128)(2,1)S(1)}, u32[]{:S(2)}, u32[]{:S(2)}) collective-permute-start(bf16[1024,512]{1,0:T(8,128)(2,1)S(1)} %fusion.3), channel_id=1, source_target_pairs={{0,124},{4,0},{8,4},{12,8},{16,12},{20,16},{24,20},{28,24},{32,28}... | collective-permute-start | bytes 3145736 | tf_op jit(solution)/shard_map/ppermute | solution.py:17
  75.8 30.3 %collective-permute-start.23 = (bf16[1024,512]{1,0:T(8,128)(2,1)S(1)}, bf16[1024,512]{1,0:T(8,128)(2,1)S(1)}, u32[]{:S(2)}, u32[]{:S(2)}) collective-permute-start(bf16[1024,512]{1,0:T(8,128)(2,1)S(1)} %fusion.3), channel_id=1, source_target_pairs={{0,4},{4,8},{8,12},{12,16},{16,20},{20,24},{24,28},{28,32},{32,36}... | collective-permute-start | bytes 3145736 | tf_op jit(solution)/shard_map/ppermute | solution.py:17
  75.9 153.3 %collective-permute-start.26 = (bf16[1024,512]{1,0:T(8,128)(2,1)S(1)}, bf16[1024,512]{1,0:T(8,128)(2,1)S(1)}, u32[]{:S(2)}, u32[]{:S(2)}) collective-permute-start(bf16[1024,512]{1,0:T(8,128)(2,1)S(1)} %fusion.2), channel_id=1, source_target_pairs={{0,124},{4,0},{8,4},{12,8},{16,12},{20,16},{24,20},{28,24},{32,28}... | collective-permute-start | bytes 3145736 | tf_op jit(solution)/shard_map/ppermute | solution.py:17
  86.9 277.4 %collective-permute-start.9 = (bf16[2048,1024]{1,0:T(8,128)(2,1)}, bf16[2048,1024]{1,0:T(8,128)(2,1)}, u32[]{:S(2)}, u32[]{:S(2)}) collective-permute-start(bf16[2048,1024]{1,0:T(8,128)(2,1)} %subtract_convert_fusion.own), channel_id=1, source_target_pairs={{0,4},{4,8},{8,12},{12,16},{16,20},{20,24},{24,28},{28,32},{32,36}... | collective-permute-start | bytes 12582920 | tf_op jit(solution)/shard_map/ppermute | solution.py:17
  86.9 277.4 %collective-permute-start.10 = (bf16[2048,1024]{1,0:T(8,128)(2,1)}, bf16[2048,1024]{1,0:T(8,128)(2,1)}, u32[]{:S(2)}, u32[]{:S(2)}) collective-permute-start(bf16[2048,1024]{1,0:T(8,128)(2,1)} %subtract_convert_fusion.own), channel_id=1, source_target_pairs={{0,124},{4,0},{8,4},{12,8},{16,12},{20,16},{24,20},{28,24},{32,28}... | collective-permute-start | bytes 12582920 | tf_op jit(solution)/shard_map/ppermute | solution.py:17
  99.7 139.2 %collective-permute-start.25 = (bf16[1024,512]{1,0:T(8,128)(2,1)S(1)}, bf16[1024,512]{1,0:T(8,128)(2,1)}, u32[]{:S(2)}, u32[]{:S(2)}) collective-permute-start(bf16[1024,512]{1,0:T(8,128)(2,1)S(1)} %fusion.2), channel_id=1, source_target_pairs={{0,4},{4,8},{8,12},{12,16},{16,20},{20,24},{24,28},{28,32},{32,36}... | collective-permute-start | bytes 3145736 | tf_op jit(solution)/shard_map/ppermute | solution.py:17
  106.1 123.1 %collective-permute-start.15 = (bf16[256,1024]{1,0:T(8,128)(2,1)S(1)}, bf16[256,1024]{1,0:T(8,128)(2,1)S(1)}, u32[]{:S(2)}, u32[]{:S(2)}) collective-permute-start(bf16[256,1024]{1,0:T(8,128)(2,1)S(1)} %fusion.16.own), channel_id=1, source_target_pairs={{0,4},{4,8},{8,12},{12,16},{16,20},{20,24},{24,28},{28,32},{32,36}... | collective-permute-start | bytes 1572872 | tf_op jit(solution)/shard_map/ppermute | solution.py:17
  229.2 128.7 %collective-permute-start.17 = (bf16[1536,1024]{1,0:T(8,128)(2,1)}, bf16[1536,1024]{1,0:T(8,128)(2,1)}, u32[]{:S(2)}, u32[]{:S(2)}) collective-permute-start(bf16[1536,1024]{1,0:T(8,128)(2,1)} %fusion.own), channel_id=1, source_target_pairs={{0,4},{4,8},{8,12},{12,16},{16,20},{20,24},{24,28},{28,32},{32,36}... | collective-permute-start | bytes 9437192 | tf_op jit(solution)/shard_map/ppermute | solution.py:17
  231.0 127.3 %collective-permute-start.18 = (bf16[1536,1024]{1,0:T(8,128)(2,1)}, bf16[1536,1024]{1,0:T(8,128)(2,1)}, u32[]{:S(2)}, u32[]{:S(2)}) collective-permute-start(bf16[1536,1024]{1,0:T(8,128)(2,1)} %fusion.own), channel_id=1, source_target_pairs={{0,124},{4,0},{8,4},{12,8},{16,12},{20,16},{24,20},{28,24},{32,28}... | collective-permute-start | bytes 9437192 | tf_op jit(solution)/shard_map/ppermute | solution.py:17
  238.9 87.1 %collective-permute-start.28 = (bf16[1024,512]{1,0:T(8,128)(2,1)S(1)}, bf16[1024,512]{1,0:T(8,128)(2,1)S(1)}, u32[]{:S(2)}, u32[]{:S(2)}) collective-permute-start(bf16[1024,512]{1,0:T(8,128)(2,1)S(1)} %fusion.1), channel_id=1, source_target_pairs={{0,124},{4,0},{8,4},{12,8},{16,12},{20,16},{24,20},{28,24},{32,28}... | collective-permute-start | bytes 3145736 | tf_op jit(solution)/shard_map/ppermute | solution.py:17
  326.0 28.5 %collective-permute-start.27 = (bf16[1024,512]{1,0:T(8,128)(2,1)S(1)}, bf16[1024,512]{1,0:T(8,128)(2,1)S(1)}, u32[]{:S(2)}, u32[]{:S(2)}) collective-permute-start(bf16[1024,512]{1,0:T(8,128)(2,1)S(1)} %fusion.1), channel_id=1, source_target_pairs={{0,4},{4,8},{8,12},{12,16},{16,20},{20,24},{24,28},{28,32},{32,36}... | collective-permute-start | bytes 3145736 | tf_op jit(solution)/shard_map/ppermute | solution.py:17
  354.5 35.0 %collective-permute-start.16 = (bf16[256,1024]{1,0:T(8,128)(2,1)S(1)}, bf16[256,1024]{1,0:T(8,128)(2,1)S(1)}, u32[]{:S(2)}, u32[]{:S(2)}) collective-permute-start(bf16[256,1024]{1,0:T(8,128)(2,1)S(1)} %copy-done.23), channel_id=1, source_target_pairs={{0,124},{4,0},{8,4},{12,8},{16,12},{20,16},{24,20},{28,24},{32,28}... | collective-permute-start | bytes 1572872 | tf_op jit(solution)/shard_map/ppermute | solution.py:17
  358.0 38.0 %collective-permute-start.11 = (bf16[128,1024]{1,0:T(8,128)(2,1)S(1)}, bf16[128,1024]{1,0:T(8,128)(2,1)S(1)}, u32[]{:S(2)}, u32[]{:S(2)}) collective-permute-start(bf16[128,1024]{1,0:T(8,128)(2,1)S(1)} %fusion.22.own), channel_id=1, source_target_pairs={{0,4},{4,8},{8,12},{12,16},{16,20},{20,24},{24,28},{28,32},{32,36}... | collective-permute-start | bytes 786440 | tf_op jit(solution)/shard_map/ppermute | solution.py:17
  358.3 37.6 %collective-permute-start.12 = (bf16[128,1024]{1,0:T(8,128)(2,1)S(1)}, bf16[128,1024]{1,0:T(8,128)(2,1)S(1)}, u32[]{:S(2)}, u32[]{:S(2)}) collective-permute-start(bf16[128,1024]{1,0:T(8,128)(2,1)S(1)} %fusion.22.own), channel_id=1, source_target_pairs={{0,124},{4,0},{8,4},{12,8},{16,12},{20,16},{24,20},{28,24},{32,28}... | collective-permute-start | bytes 786440 | tf_op jit(solution)/shard_map/ppermute | solution.py:17
  364.3 28.3 %collective-permute-start.13 = (bf16[128,1024]{1,0:T(8,128)(2,1)}, bf16[128,1024]{1,0:T(8,128)(2,1)S(1)}, u32[]{:S(2)}, u32[]{:S(2)}) collective-permute-start(bf16[128,1024]{1,0:T(8,128)(2,1)} %fusion.21.own), channel_id=1, source_target_pairs={{0,4},{4,8},{8,12},{12,16},{16,20},{20,24},{24,28},{28,32},{32,36}... | collective-permute-start | bytes 786440 | tf_op jit(solution)/shard_map/ppermute | solution.py:17
  364.3 28.3 %collective-permute-start.14 = (bf16[128,1024]{1,0:T(8,128)(2,1)}, bf16[128,1024]{1,0:T(8,128)(2,1)S(1)}, u32[]{:S(2)}, u32[]{:S(2)}) collective-permute-start(bf16[128,1024]{1,0:T(8,128)(2,1)} %fusion.21.own), channel_id=1, source_target_pairs={{0,124},{4,0},{8,4},{12,8},{16,12},{20,16},{24,20},{28,24},{32,28}... | collective-permute-start | bytes 786440 | tf_op jit(solution)/shard_map/ppermute | solution.py:17
  (45 other events, 678.5 us)

commit v2 on v1

v2 whole, which is shorter than its diff:
```python
import jax
import jax.numpy as jnp
from jax import lax
from jax.experimental import pallas as pl
from jax.experimental.pallas import tpu as pltpu
from jax.sharding import PartitionSpec as P


SIZES = (256, 640, 128)
UP_ROWS = (1536, 256, 128, 128)
BLOCK = 256
MIB = 1024 * 1024


def exchange(value, parity):
    count = lax.axis_size("gossip")
    pairs = [(s, (s + 1 if s % 2 == parity else s - 1) % count) for s in range(count)]
    return lax.ppermute(value, "gossip", pairs)


def other_core(value):
    count = lax.axis_size("mp")
    return lax.ppermute(value, "mp", [(s, s ^ 1) for s in range(count)])


def other_chip(value):
    count = lax.axis_size("mp")
    return lax.ppermute(value, "mp", [(s, s ^ 2) for s in range(count)])


def both_ways(value):
    first = exchange(value, 1)
    second = exchange(value, 0)
    return first, value, second


def mix_three(lower, own, upper):
    total = lower.astype(jnp.float32) + own.astype(jnp.float32) + upper.astype(jnp.float32)
    return (total / 3.0).astype(jnp.bfloat16)


def mix_rows(before, rows_out, start, parts):
    rows, width = parts[1].shape
    block = min(rows, 256)

    def body(lower, own, upper, *rest):
        rest[-1][...] = mix_three(lower[...], own[...], upper[...])

    piece = pl.BlockSpec((block, width), lambda n: (n, 0))
    extra = [] if before is None else [before]
    return pl.pallas_call(
        body,
        grid=(rows // block,),
        in_specs=[piece] * 3 + [pl.BlockSpec(memory_space=pl.ANY)] * len(extra),
        out_specs=pl.BlockSpec((block, width), lambda n: (start // block + n, 0)),
        out_shape=jax.ShapeDtypeStruct((rows_out, width), jnp.bfloat16),
        input_output_aliases={3: 0} if start else {},
        compiler_params=pltpu.CompilerParams(vmem_limit_bytes=(56 if rows > 256 else 4) * MIB),
    )(*parts, *extra)


def dot(a, b, dims):
    return lax.dot_general(a, b, (dims, ((), ())), preferred_element_type=jnp.float32)


def forward_body(core, *refs, in_scale):
    tokens, w_gate, w_up, w_down = refs[:4]
    outs = refs[4 : 8 + len(SIZES)]
    (
        tok, gate_v, up_v, down_t, hidden, hidden_t, slope, act, theirs, in_sems, out_sems,
    ) = refs[8 + len(SIZES) :]
    _, width = tok.shape
    half = width // 2
    blocks = hidden.shape[1] // BLOCK
    at_theirs = pl.multiple_of((1 - core[0]) * half, half)
    done = []

    def fetch(n, src, dst):
        return pltpu.make_async_copy(src, dst, in_sems.at[n])

    def put(src, dst):
        copy = pltpu.make_async_copy(src, dst, out_sems.at[len(done)])
        copy.start()
        done.append(copy)

    def span(n):
        return slice(n * BLOCK, (n + 1) * BLOCK)

    tok_copy = fetch(0, tokens, tok)
    weight_copies = [
        (
            fetch(1 + 2 * n, w_gate.at[:, span(n)], gate_v.at[:, span(n)]),
            fetch(2 + 2 * n, w_up.at[:, span(n)], up_v.at[:, span(n)]),
        )
        for n in range(blocks)
    ]
    copy_t = fetch(1 + 2 * blocks, w_down.at[:, pl.ds(at_theirs, half)], down_t)
    for copy in (tok_copy, *weight_copies[0]):
        copy.start()
    tok_copy.wait()
    for copy in weight_copies[1]:
        copy.start()
    for n in range(blocks):
        if n + 2 < blocks:
            for copy in weight_copies[n + 2]:
                copy.start()
        elif n + 2 == blocks:
            copy_t.start()
        for copy in weight_copies[n]:
            copy.wait()
        if n == 0:
            wide = tok[...].astype(jnp.float32)
            scale = lax.rsqrt(jnp.mean(wide * wide, axis=-1, keepdims=True) + 1e-06)
        cols = span(n)
        gate_pre = jnp.dot(tok[...], gate_v[:, cols], preferred_element_type=jnp.float32)
        up_pre = jnp.dot(tok[...], up_v[:, cols], preferred_element_type=jnp.float32)
        gate_pre = gate_pre * (scale * in_scale)
        up_pre = up_pre * (scale * in_scale)
        sig = jax.nn.sigmoid(gate_pre)
        activated = gate_pre * sig
        value = (activated * up_pre).astype(jnp.bfloat16)
        hidden[:, cols] = value
        hidden_t[cols] = value.T
        act[:, cols] = (activated * scale).astype(jnp.bfloat16)
        slope[:, cols] = (up_pre * (sig * (1.0 + gate_pre * (1.0 - sig))) * scale).astype(
            jnp.bfloat16
        )
        put(hidden.at[:, cols], outs[0].at[:, cols])
        put(hidden_t.at[cols], outs[1].at[cols])
        put(slope.at[:, cols], outs[2].at[:, cols])
        put(act.at[:, cols], outs[3].at[:, cols])
    copy_t.wait()
    at = 0
    for n, size in enumerate(SIZES):
        cols = slice(at, at + size)
        theirs[:, cols] = jnp.dot(
            hidden[...], down_t[:, cols], preferred_element_type=jnp.float32
        ).astype(jnp.bfloat16)
        put(theirs.at[:, cols], outs[4 + n])
        at += size
    for copy in done:
        copy.wait()


def forward(core, tokens, w_gate, w_up, w_down, in_scale):
    rows, width = tokens.shape
    count = w_gate.shape[1]
    half = width // 2
    anywhere = pl.BlockSpec(memory_space=pl.ANY)
    shapes = [(rows, count), (count, rows), (rows, count), (rows, count)]
    outs = [
        jax.ShapeDtypeStruct(shape, jnp.bfloat16)
        for shape in shapes + [(rows, size) for size in SIZES]
    ]
    blocks = count // BLOCK
    return pl.pallas_call(
        lambda *refs: forward_body(*refs, in_scale=in_scale),
        name="forward",
        in_specs=[pl.BlockSpec(memory_space=pltpu.SMEM)] + [anywhere] * 4,
        out_specs=[anywhere] * len(outs),
        out_shape=outs,
        scratch_shapes=[
            pltpu.VMEM((rows, width), jnp.bfloat16),
            pltpu.VMEM((width, count), jnp.bfloat16),
            pltpu.VMEM((width, count), jnp.bfloat16),
            pltpu.VMEM((count, half), jnp.bfloat16),
            *[pltpu.VMEM(shape, jnp.bfloat16) for shape in shapes],
            pltpu.VMEM((rows, half), jnp.bfloat16),
            pltpu.SemaphoreType.DMA((2 + 2 * blocks,)),
            pltpu.SemaphoreType.DMA((4 * blocks + len(SIZES),)),
        ],
        compiler_params=pltpu.CompilerParams(vmem_limit_bytes=58 * MIB),
    )(core[None].astype(jnp.int32), tokens, w_gate, w_up, w_down)


def compute(tokens, targets, gate_weight, up_weight, down_weight):
    inputs = tokens[0]
    wanted = targets[0]
    w_gate = gate_weight[0]
    w_up = up_weight[0]
    w_down = down_weight[0]
    tok_count, width = inputs.shape
    mp_count = lax.axis_size("mp")
    hidden_all = w_gate.shape[1] * mp_count
    in_scale = 1.0 / width**0.5
    mid_scale = 1.0 / hidden_all**0.5
    step_size = hidden_all / 4.0
    half = width // 2
    core = lax.axis_index("mp") % 2
    mine = core * half
    theirs = half - mine

    outs = forward(core, inputs, w_gate, w_up, w_down, in_scale)
    hidden, hidden_t, slope_gate, act = outs[:4]
    sums_theirs = outs[4:]

    def columns(array, start, size):
        return lax.dynamic_slice_in_dim(array, start, size, 1)

    def stepped_down(err, start):
        grad = dot(hidden_t, err, ((1,), (0,))) * mid_scale
        w_piece = columns(w_down, start, err.shape[1])
        new = (w_piece.astype(jnp.float32) - step_size * grad).astype(jnp.bfloat16)
        down_parts.append((start, both_ways(new)))

    totals = []
    far = []
    at = 0
    for n, size in enumerate(SIZES):
        arrived = other_core(sums_theirs[n])
        own = dot(hidden, columns(w_down, mine + at, size), ((1,), (0,)))
        own = lax.optimization_barrier(own)
        total = own + arrived.astype(jnp.float32)
        rounded = total.astype(jnp.bfloat16)
        totals.append(total)
        far.append(other_chip(rounded))
        at += size

    err_mine = []
    err_theirs = []
    down_parts = []
    at = 0
    for n, size in enumerate(SIZES):
        output = (totals[n] + far[n].astype(jnp.float32)) * mid_scale
        offset = columns(inputs, mine + at, size).astype(jnp.float32) - columns(
            wanted, mine + at, size
        ).astype(jnp.float32)
        err = ((offset + output) / tok_count).astype(jnp.bfloat16)
        err_mine.append(err)
        err_theirs.append(other_core(err))
        stepped_down(err, mine + at)
        at += size
    err_t = jnp.concatenate(err_theirs, 1)
    stepped_down(err_t, theirs)

    grad_hidden = dot(
        jnp.concatenate(err_mine, 1), columns(w_down, mine, half), ((1,), (1,))
    ) + dot(err_t, columns(w_down, theirs, half), ((1,), (1,)))
    grad_hidden = grad_hidden * mid_scale
    grad_gate = (grad_hidden * slope_gate.astype(jnp.float32)).astype(jnp.bfloat16)
    grad_up = (grad_hidden * act.astype(jnp.float32)).astype(jnp.bfloat16)

    def stepped(weight, grad_in, row, rows):
        grad_w = dot(inputs[:, row : row + rows], grad_in, ((0,), (0,))) * in_scale
        new = (weight[row : row + rows].astype(jnp.float32) - step_size * grad_w).astype(
            jnp.bfloat16
        )
        return both_ways(new)

    gate_parts = stepped(w_gate, grad_gate, 0, width)
    up_parts = []
    row = 0
    for rows in UP_ROWS:
        up_parts.append((row, stepped(w_up, grad_up, row, rows)))
        row += rows

    down_out = jnp.zeros_like(w_down)
    for start, parts in down_parts:
        down_out = lax.dynamic_update_slice(down_out, mix_three(*parts), (0, start))
    gate_out = mix_rows(None, width, 0, gate_parts)
    up_out = gate_out[:16]
    for start, parts in up_parts:
        up_out = mix_rows(up_out, width, start, parts)
    return gate_out[None], up_out[None], down_out[None]


def solution(mesh):
    placed = (
        P("gossip", None, None),
        P("gossip", None, None),
        P("gossip", None, "mp"),
        P("gossip", None, "mp"),
        P("gossip", "mp", None),
    )
    return jax.shard_map(
        compute,
        mesh=mesh,
        in_specs=placed,
        out_specs=(P("gossip", None, "mp"), P("gossip", None, "mp"), P("gossip", "mp", None)),
        check_vma=False,
    )
```

time: 400 us -> 359 us (0.90)
  waiting for transfers between devices: 269 us -> 234 us
  starting transfers between devices: 56.8 us -> 49.2 us
  other arithmetic: 7.57 us -> 12.9 us
  Pallas kernels: 35.7 us -> 30.7 us
    ppermute x20 -> x18, waiting for transfers between devices: 240 us -> 220 us  [exchange(): return lax.ppermute(value, 'gossip', pairs)]
    ppermute x3, waiting for transfers between devices: 27.4 us -> 14.4 us  [other_chip(): return lax.ppermute(value, 'mp', [(s, s ^ 2) for s in range(count)])]
    ppermute x20 -> x18, starting transfers between devices: 49.3 us -> 40.6 us  [exchange(): return lax.ppermute(value, 'gossip', pairs)]
    dot_general x12 -> x14, matrix products: 21.1 us -> 21 us  [dot(): lax.dot_general(a, b, (dims, ((), ())), preferred_element_type=jnp.float32)]
  transfers between devices with their start and end apart: 29 -> 27, of which waited for: 8 -> 4; matrix products, arithmetic and copies ran while one was open for 8% -> 10% of each run, Pallas kernels for 5% -> 5%
where the time goes in v2:
time: 359 us; the launch traced here: 358 us
  waiting for transfers between devices  234 us (65%)
  starting transfers between devices  49.2 us (14%)
  Pallas kernels  30.7 us (9%)
  matrix products  21 us (6%)
  other arithmetic  12.9 us (4%)
  local copies, waits for them, and re-layouts  8.6 us (2%)
    ppermute x18, waiting for transfers between devices, exchange(): return lax.ppermute(value, 'gossip', pairs)  220 us
    ppermute x18, starting transfers between devices, exchange(): return lax.ppermute(value, 'gossip', pairs)  40.6 us
    dot_general x14, matrix products, dot(): lax.dot_general(a, b, (dims, ((), ())), preferred_element_type=jnp.float32)  21 us
    pallas_call x5, Pallas kernels, mix_rows(): pl.pallas_call(body, grid=(rows // block,), in_specs=[piece] * 3 + [pl.Bl...  19.6 us
    ppermute x3, waiting for transfers between devices, other_chip(): return lax.ppermute(value, 'mp', [(s, s ^ 2) for s in range(count)])  14.4 us
    pallas_call x1, Pallas kernels, forward(): pl.pallas_call(lambda *refs: forward_body(*refs, in_scale=in_scale), name...  11 us
  transfers between devices with their start and end apart: 27, of which 4 were waited for; matrix products, arithmetic and copies ran while one was open for 10% of the time, Pallas kernels for 5%

profile of v2, /device:TPU:0, one launch (start us, length us, event | category | flops | bytes accessed | tf_op | source)
XLA Modules:
  0.0 358.0 jit_solution(7436059033904132487)
XLA Ops:
  0.6 11.0 %forward.1 = (bf16[512,1024]{1,0:T(8,128)(2,1)}, bf16[1024,512]{1,0:T(8,128)(2,1)}, bf16[512,1024]{1,0:T(8,128)(2,1)}, bf16[512,1024]{1,0:T(8,128)(2,1)}, bf16[5...) custom-call(s32[1]{0:T(128)} %bitcast.2.refs_0_, bf16[512,2048]{1,0:T(8,128)(2,1)} %bitcast.121, ...), custom_call_target="tpu_custom_call" | custom-call | tf_op jit(solution)/shard_map/forward/pallas_call | solution.py:156
  14.2 2.7 fusion.18
  16.9 2.1 fusion.50
  20.2 3.4 collective-permute-start.5
  25.0 3.4 collective-permute-start.3
  31.2 6.6 %collective-permute-start.23 = (bf16[1024,128]{1,0:T(8,128)(2,1)S(1)}, bf16[1024,128]{1,0:T(8,128)(2,1)S(1)}, u32[]{:S(2)}, u32[]{:S(2)}) collective-permute-start(bf16[1024,128]{1,0:T(8,128)(2,1)S(1)} %fusion.29), channel_id=1, source_target_pairs={{0,124},{4,8},{8,4},{12,16},{16,12},{20,24},{24,20},{28,32},{32,28... | collective-permute-start | bytes 786440 | tf_op jit(solution)/shard_map/ppermute | solution.py:18
  39.8 14.4 %collective-permute-done.3 = bf16[512,640]{1,0:T(8,128)(2,1)S(1)} collective-permute-done((bf16[512,640]{1,0:T(8,128)(2,1)S(1)}, bf16[512,640]{1,0:T(8,128)(2,1)S(1)}, u32[]{:S(2)}, u32[]{:S(2)}) %collective-permute-start.3) | collective-permute-done | bytes 655392 | tf_op jit(solution)/shard_map/ppermute | solution.py:28
  56.4 6.4 %collective-permute-start.19 = (bf16[1024,256]{1,0:T(8,128)(2,1)S(1)}, bf16[1024,256]{1,0:T(8,128)(2,1)S(1)}, u32[]{:S(2)}, u32[]{:S(2)}) collective-permute-start(bf16[1024,256]{1,0:T(8,128)(2,1)S(1)} %fusion.23), channel_id=1, source_target_pairs={{0,124},{4,8},{8,4},{12,16},{16,12},{20,24},{24,20},{28,32},{32,28... | collective-permute-start | bytes 1572872 | tf_op jit(solution)/shard_map/ppermute | solution.py:18
  68.3 2.0 copy-done.3
  70.8 2.1 collective-permute-start.22
  72.9 4.3 %collective-permute-start.25 = (bf16[1024,1024]{1,0:T(8,128)(2,1)S(1)}, bf16[1024,1024]{1,0:T(8,128)(2,1)S(1)}, u32[]{:S(2)}, u32[]{:S(2)}) collective-permute-start(bf16[1024,1024]{1,0:T(8,128)(2,1)S(1)} %subtract_convert_fusion), channel_id=1, source_target_pairs={{0,124},{4,8},{8,4},{12,16},{16,12},{20,24},{24,20},{28,32},{32,28... | collective-permute-start | bytes 6291464 | tf_op jit(solution)/shard_map/ppermute | solution.py:18
  77.2 4.6 %collective-permute-start.15 = (bf16[256,1024]{1,0:T(8,128)(2,1)S(1)}, bf16[256,1024]{1,0:T(8,128)(2,1)S(1)}, u32[]{:S(2)}, u32[]{:S(2)}) collective-permute-start(bf16[256,1024]{1,0:T(8,128)(2,1)S(1)} %fusion.22.own), channel_id=1, source_target_pairs={{0,124},{4,8},{8,4},{12,16},{16,12},{20,24},{24,20},{28,32},{32,28... | collective-permute-start | bytes 1572872 | tf_op jit(solution)/shard_map/ppermute | solution.py:18
  81.8 2.8 fusion.own
  84.8 74.8 %collective-permute-done.15.lower = bf16[256,1024]{1,0:T(8,128)(2,1)S(1)} collective-permute-done((bf16[256,1024]{1,0:T(8,128)(2,1)S(1)}, bf16[256,1024]{1,0:T(8,128)(2,1)S(1)}, u32[]{:S(2)}, u32[]{:S(2)}) %collective-permute-start.15) | collective-permute-done | bytes 524320 | tf_op jit(solution)/shard_map/ppermute | solution.py:18
  159.6 6.0 %collective-permute-start.9 = (bf16[2048,1024]{1,0:T(8,128)(2,1)S(1)}, bf16[2048,1024]{1,0:T(8,128)(2,1)S(1)}, u32[]{:S(2)}, u32[]{:S(2)}) collective-permute-start(bf16[2048,1024]{1,0:T(8,128)(2,1)S(1)} %fusion.own), channel_id=1, source_target_pairs={{0,124},{4,8},{8,4},{12,16},{16,12},{20,24},{24,20},{28,32},{32,28... | collective-permute-start | bytes 12582920 | tf_op jit(solution)/shard_map/ppermute | solution.py:18
  165.6 3.3 fusion.1.own
  175.0 2.1 fusion.17
  177.1 132.5 %collective-permute-done.26 = bf16[1024,1024]{1,0:T(8,128)(2,1)} collective-permute-done((bf16[1024,1024]{1,0:T(8,128)(2,1)S(1)}, bf16[1024,1024]{1,0:T(8,128)(2,1)}, u32[]{:S(2)}, u32[]{:S(2)}) %collective-permute-start.26) | collective-permute-done | bytes 2097184 | tf_op jit(solution)/shard_map/ppermute | solution.py:18
  311.1 12.5 %collective-permute-done.17.lower = bf16[1536,1024]{1,0:T(8,128)(2,1)S(1)} collective-permute-done((bf16[1536,1024]{1,0:T(8,128)(2,1)S(1)}, bf16[1536,1024]{1,0:T(8,128)(2,1)S(1)}, u32[]{:S(2)}, u32[]{:S(2)}) %collective-permute-start.17) | collective-permute-done | bytes 3145760 | tf_op jit(solution)/shard_map/ppermute | solution.py:18
  323.6 5.7 %collective-permute-start.13 = (bf16[128,1024]{1,0:T(8,128)(2,1)S(1)}, bf16[128,1024]{1,0:T(8,128)(2,1)S(1)}, u32[]{:S(2)}, u32[]{:S(2)}) collective-permute-start(bf16[128,1024]{1,0:T(8,128)(2,1)S(1)} %fusion.30.own), channel_id=1, source_target_pairs={{0,124},{4,8},{8,4},{12,16},{16,12},{20,24},{24,20},{28,32},{32,28... | collective-permute-start | bytes 786440 | tf_op jit(solution)/shard_map/ppermute | solution.py:18
  331.4 2.0 collective-permute-start.12
  333.7 3.1 fusion.3
  336.9 10.1 %shard_map.76 = bf16[2048,1024]{1,0:T(8,128)(2,1)} custom-call(bf16[2048,1024]{1,0:T(8,128)(2,1)} %copy-done.8, bf16[2048,1024]{1,0:T(8,128)(2,1)} %copy-done.6, bf16[2048,1024]{1,0:T(8,128)(2,1)} %copy-done.7), custom_call_target="tpu_custom_call" | custom-call | tf_op jit(solution)/shard_map/pallas_call | solution.py:51
  348.4 6.9 %shard_map.77.rest_0_ = bf16[2048,1024]{1,0:T(8,128)(2,1)} custom-call(bf16[1536,1024]{1,0:T(8,128)(2,1)} %copy-done.10, bf16[1536,1024]{1,0:T(8,128)(2,1)} %copy-done.9, bf16[1536,1024]{1,0:T(8,128)(2,1)} %copy-done.11, bf16[16,1024]{1,0:T(8,128)(2,1)} %slice.44.rest_0_), custom_call_target="tpu_custom_call" | custom-call | tf_op jit(solution)/shard_map/pallas_call | solution.py:51
  (129 shorter events, 31.8 us)
Async XLA Ops:
  11.7 11.9 %collective-permute-start = (bf16[512,256]{1,0:T(8,128)(2,1)}, bf16[512,256]{1,0:T(8,128)(2,1)}, u32[]{:S(2)}, u32[]{:S(2)}) collective-permute-start(bf16[512,256]{1,0:T(8,128)(2,1)} %get-tuple-element.11), channel_id=1, source_target_pairs={{0,1},{1,0},{2,3},{3,2},{4,5},{5,4},{6,7},{7,6},{8,9},{9,8},{10,11... | collective-permute-start | bytes 786440 | tf_op jit(solution)/shard_map/ppermute | solution.py:23
  11.8 13.1 %collective-permute-start.2 = (bf16[512,640]{1,0:T(8,128)(2,1)}, bf16[512,640]{1,0:T(8,128)(2,1)S(1)}, u32[]{:S(2)}, u32[]{:S(2)}) collective-permute-start(bf16[512,640]{1,0:T(8,128)(2,1)} %get-tuple-element.12), channel_id=1, source_target_pairs={{0,1},{1,0},{2,3},{3,2},{4,5},{5,4},{6,7},{7,6},{8,9},{9,8},{10,11... | collective-permute-start | bytes 1966088 | tf_op jit(solution)/shard_map/ppermute | solution.py:23
  24.6 13.2 %collective-permute-start.1 = (bf16[512,256]{1,0:T(8,128)(2,1)S(1)}, bf16[512,256]{1,0:T(8,128)(2,1)S(1)}, u32[]{:S(2)}, u32[]{:S(2)}) collective-permute-start(bf16[512,256]{1,0:T(8,128)(2,1)S(1)} %fusion.46), channel_id=1, source_target_pairs={{0,2},{1,3},{2,0},{3,1},{4,6},{5,7},{6,4},{7,5},{8,10},{9,11},{10,... | collective-permute-start | bytes 786440 | tf_op jit(solution)/shard_map/ppermute | solution.py:28
  25.0 29.2 %collective-permute-start.3 = (bf16[512,640]{1,0:T(8,128)(2,1)S(1)}, bf16[512,640]{1,0:T(8,128)(2,1)S(1)}, u32[]{:S(2)}, u32[]{:S(2)}) collective-permute-start(bf16[512,640]{1,0:T(8,128)(2,1)S(1)} %fusion.38), channel_id=1, source_target_pairs={{0,2},{1,3},{2,0},{3,1},{4,6},{5,7},{6,4},{7,5},{8,10},{9,11},{10,... | collective-permute-start | bytes 1966088 | tf_op jit(solution)/shard_map/ppermute | solution.py:28
  31.2 39.5 %collective-permute-start.23 = (bf16[1024,128]{1,0:T(8,128)(2,1)S(1)}, bf16[1024,128]{1,0:T(8,128)(2,1)S(1)}, u32[]{:S(2)}, u32[]{:S(2)}) collective-permute-start(bf16[1024,128]{1,0:T(8,128)(2,1)S(1)} %fusion.29), channel_id=1, source_target_pairs={{0,124},{4,8},{8,4},{12,16},{16,12},{20,24},{24,20},{28,32},{32,28... | collective-permute-start | bytes 786440 | tf_op jit(solution)/shard_map/ppermute | solution.py:18
  37.8 35.0 %collective-permute-start.24 = (bf16[1024,128]{1,0:T(8,128)(2,1)S(1)}, bf16[1024,128]{1,0:T(8,128)(2,1)}, u32[]{:S(2)}, u32[]{:S(2)}) collective-permute-start(bf16[1024,128]{1,0:T(8,128)(2,1)S(1)} %fusion.29), channel_id=1, source_target_pairs={{0,4},{4,0},{8,12},{12,8},{16,20},{20,16},{24,28},{28,24},{32,36},... | collective-permute-start | bytes 786440 | tf_op jit(solution)/shard_map/ppermute | solution.py:18
  37.8 27.6 %collective-permute-start.8 = (bf16[512,128]{1,0:T(8,128)(2,1)S(1)}, bf16[512,128]{1,0:T(8,128)(2,1)S(1)}, u32[]{:S(2)}, u32[]{:S(2)}) collective-permute-start(bf16[512,128]{1,0:T(8,128)(2,1)S(1)} %fusion.53), channel_id=1, source_target_pairs={{0,1},{1,0},{2,3},{3,2},{4,5},{5,4},{6,7},{7,6},{8,9},{9,8},{10,11... | collective-permute-start | bytes 393224 | tf_op jit(solution)/shard_map/ppermute | solution.py:23
  39.1 17.3 %collective-permute-start.6 = (bf16[512,256]{1,0:T(8,128)(2,1)S(1)}, bf16[512,256]{1,0:T(8,128)(2,1)S(1)}, u32[]{:S(2)}, u32[]{:S(2)}) collective-permute-start(bf16[512,256]{1,0:T(8,128)(2,1)S(1)} %fusion.44), channel_id=1, source_target_pairs={{0,1},{1,0},{2,3},{3,2},{4,5},{5,4},{6,7},{7,6},{8,9},{9,8},{10,11... | collective-permute-start | bytes 786440 | tf_op jit(solution)/shard_map/ppermute | solution.py:23
  56.4 20.8 %collective-permute-start.19 = (bf16[1024,256]{1,0:T(8,128)(2,1)S(1)}, bf16[1024,256]{1,0:T(8,128)(2,1)S(1)}, u32[]{:S(2)}, u32[]{:S(2)}) collective-permute-start(bf16[1024,256]{1,0:T(8,128)(2,1)S(1)} %fusion.23), channel_id=1, source_target_pairs={{0,124},{4,8},{8,4},{12,16},{16,12},{20,24},{24,20},{28,32},{32,28... | collective-permute-start | bytes 1572872 | tf_op jit(solution)/shard_map/ppermute | solution.py:18
  65.1 19.5 %collective-permute-start.20 = (bf16[1024,256]{1,0:T(8,128)(2,1)S(1)}, bf16[1024,256]{1,0:T(8,128)(2,1)S(1)}, u32[]{:S(2)}, u32[]{:S(2)}) collective-permute-start(bf16[1024,256]{1,0:T(8,128)(2,1)S(1)} %fusion.23), channel_id=1, source_target_pairs={{0,4},{4,0},{8,12},{12,8},{16,20},{20,16},{24,28},{28,24},{32,36},... | collective-permute-start | bytes 1572872 | tf_op jit(solution)/shard_map/ppermute | solution.py:18
  65.4 103.6 %collective-permute-start.21 = (bf16[1024,640]{1,0:T(8,128)(2,1)S(1)}, bf16[1024,640]{1,0:T(8,128)(2,1)S(1)}, u32[]{:S(2)}, u32[]{:S(2)}) collective-permute-start(bf16[1024,640]{1,0:T(8,128)(2,1)S(1)} %subtract_convert_fusion.1), channel_id=1, source_target_pairs={{0,124},{4,8},{8,4},{12,16},{16,12},{20,24},{24,20},{28,32},{32,28... | collective-permute-start | bytes 3932168 | tf_op jit(solution)/shard_map/ppermute | solution.py:18
  70.8 98.6 %collective-permute-start.22 = (bf16[1024,640]{1,0:T(8,128)(2,1)S(1)}, bf16[1024,640]{1,0:T(8,128)(2,1)}, u32[]{:S(2)}, u32[]{:S(2)}) collective-permute-start(bf16[1024,640]{1,0:T(8,128)(2,1)S(1)} %subtract_convert_fusion.1), channel_id=1, source_target_pairs={{0,4},{4,0},{8,12},{12,8},{16,20},{20,16},{24,28},{28,24},{32,36},... | collective-permute-start | bytes 3932168 | tf_op jit(solution)/shard_map/ppermute | solution.py:18
  72.9 96.5 %collective-permute-start.25 = (bf16[1024,1024]{1,0:T(8,128)(2,1)S(1)}, bf16[1024,1024]{1,0:T(8,128)(2,1)S(1)}, u32[]{:S(2)}, u32[]{:S(2)}) collective-permute-start(bf16[1024,1024]{1,0:T(8,128)(2,1)S(1)} %subtract_convert_fusion), channel_id=1, source_target_pairs={{0,124},{4,8},{8,4},{12,16},{16,12},{20,24},{24,20},{28,32},{32,28... | collective-permute-start | bytes 6291464 | tf_op jit(solution)/shard_map/ppermute | solution.py:18
  77.2 82.4 %collective-permute-start.15 = (bf16[256,1024]{1,0:T(8,128)(2,1)S(1)}, bf16[256,1024]{1,0:T(8,128)(2,1)S(1)}, u32[]{:S(2)}, u32[]{:S(2)}) collective-permute-start(bf16[256,1024]{1,0:T(8,128)(2,1)S(1)} %fusion.22.own), channel_id=1, source_target_pairs={{0,124},{4,8},{8,4},{12,16},{16,12},{20,24},{24,20},{28,32},{32,28... | collective-permute-start | bytes 1572872 | tf_op jit(solution)/shard_map/ppermute | solution.py:18
  84.7 244.7 %collective-permute-start.10 = (bf16[2048,1024]{1,0:T(8,128)(2,1)S(1)}, bf16[2048,1024]{1,0:T(8,128)(2,1)S(1)}, u32[]{:S(2)}, u32[]{:S(2)}) collective-permute-start(bf16[2048,1024]{1,0:T(8,128)(2,1)S(1)} %fusion.own), channel_id=1, source_target_pairs={{0,4},{4,0},{8,12},{12,8},{16,20},{20,16},{24,28},{28,24},{32,36},... | collective-permute-start | bytes 12582920 | tf_op jit(solution)/shard_map/ppermute | solution.py:18
  159.6 170.4 %collective-permute-start.9 = (bf16[2048,1024]{1,0:T(8,128)(2,1)S(1)}, bf16[2048,1024]{1,0:T(8,128)(2,1)S(1)}, u32[]{:S(2)}, u32[]{:S(2)}) collective-permute-start(bf16[2048,1024]{1,0:T(8,128)(2,1)S(1)} %fusion.own), channel_id=1, source_target_pairs={{0,124},{4,8},{8,4},{12,16},{16,12},{20,24},{24,20},{28,32},{32,28... | collective-permute-start | bytes 12582920 | tf_op jit(solution)/shard_map/ppermute | solution.py:18
  169.0 154.6 %collective-permute-start.17 = (bf16[1536,1024]{1,0:T(8,128)(2,1)S(1)}, bf16[1536,1024]{1,0:T(8,128)(2,1)S(1)}, u32[]{:S(2)}, u32[]{:S(2)}) collective-permute-start(bf16[1536,1024]{1,0:T(8,128)(2,1)S(1)} %fusion.1.own), channel_id=1, source_target_pairs={{0,124},{4,8},{8,4},{12,16},{16,12},{20,24},{24,20},{28,32},{32,28... | collective-permute-start | bytes 9437192 | tf_op jit(solution)/shard_map/ppermute | solution.py:18
  169.4 160.0 %collective-permute-start.18 = (bf16[1536,1024]{1,0:T(8,128)(2,1)S(1)}, bf16[1536,1024]{1,0:T(8,128)(2,1)S(1)}, u32[]{:S(2)}, u32[]{:S(2)}) collective-permute-start(bf16[1536,1024]{1,0:T(8,128)(2,1)S(1)} %fusion.1.own), channel_id=1, source_target_pairs={{0,4},{4,0},{8,12},{12,8},{16,20},{20,16},{24,28},{28,24},{32,36},... | collective-permute-start | bytes 9437192 | tf_op jit(solution)/shard_map/ppermute | solution.py:18
  171.4 138.3 %collective-permute-start.26 = (bf16[1024,1024]{1,0:T(8,128)(2,1)S(1)}, bf16[1024,1024]{1,0:T(8,128)(2,1)}, u32[]{:S(2)}, u32[]{:S(2)}) collective-permute-start(bf16[1024,1024]{1,0:T(8,128)(2,1)S(1)} %subtract_convert_fusion), channel_id=1, source_target_pairs={{0,4},{4,0},{8,12},{12,8},{16,20},{20,16},{24,28},{28,24},{32,36},... | collective-permute-start | bytes 6291464 | tf_op jit(solution)/shard_map/ppermute | solution.py:18
  309.7 45.6 %collective-permute-start.16 = (bf16[256,1024]{1,0:T(8,128)(2,1)S(1)}, bf16[256,1024]{1,0:T(8,128)(2,1)S(1)}, u32[]{:S(2)}, u32[]{:S(2)}) collective-permute-start(bf16[256,1024]{1,0:T(8,128)(2,1)S(1)} %fusion.22.own), channel_id=1, source_target_pairs={{0,4},{4,0},{8,12},{12,8},{16,20},{20,16},{24,28},{28,24},{32,36},... | collective-permute-start | bytes 1572872 | tf_op jit(solution)/shard_map/ppermute | solution.py:18
  323.6 32.7 %collective-permute-start.13 = (bf16[128,1024]{1,0:T(8,128)(2,1)S(1)}, bf16[128,1024]{1,0:T(8,128)(2,1)S(1)}, u32[]{:S(2)}, u32[]{:S(2)}) collective-permute-start(bf16[128,1024]{1,0:T(8,128)(2,1)S(1)} %fusion.30.own), channel_id=1, source_target_pairs={{0,124},{4,8},{8,4},{12,16},{16,12},{20,24},{24,20},{28,32},{32,28... | collective-permute-start | bytes 786440 | tf_op jit(solution)/shard_map/ppermute | solution.py:18
  329.3 27.0 %collective-permute-start.14 = (bf16[128,1024]{1,0:T(8,128)(2,1)S(1)}, bf16[128,1024]{1,0:T(8,128)(2,1)S(1)}, u32[]{:S(2)}, u32[]{:S(2)}) collective-permute-start(bf16[128,1024]{1,0:T(8,128)(2,1)S(1)} %fusion.30.own), channel_id=1, source_target_pairs={{0,4},{4,0},{8,12},{12,8},{16,20},{20,16},{24,28},{28,24},{32,36},... | collective-permute-start | bytes 786440 | tf_op jit(solution)/shard_map/ppermute | solution.py:18
  329.3 27.8 %collective-permute-start.11 = (bf16[128,1024]{1,0:T(8,128)(2,1)S(1)}, bf16[128,1024]{1,0:T(8,128)(2,1)S(1)}, u32[]{:S(2)}, u32[]{:S(2)}) collective-permute-start(bf16[128,1024]{1,0:T(8,128)(2,1)S(1)} %fusion.31.own), channel_id=1, source_target_pairs={{0,124},{4,8},{8,4},{12,16},{16,12},{20,24},{24,20},{28,32},{32,28... | collective-permute-start | bytes 786440 | tf_op jit(solution)/shard_map/ppermute | solution.py:18
  331.4 25.8 %collective-permute-start.12 = (bf16[128,1024]{1,0:T(8,128)(2,1)S(1)}, bf16[128,1024]{1,0:T(8,128)(2,1)S(1)}, u32[]{:S(2)}, u32[]{:S(2)}) collective-permute-start(bf16[128,1024]{1,0:T(8,128)(2,1)S(1)} %fusion.31.own), channel_id=1, source_target_pairs={{0,4},{4,0},{8,12},{12,8},{16,20},{20,16},{24,28},{28,24},{32,36},... | collective-permute-start | bytes 786440 | tf_op jit(solution)/shard_map/ppermute | solution.py:18
  (35 other events, 767.7 us)

commit v3 on v2

--- a/solution.py
+++ b/solution.py
@@ -6,9 +6,11 @@
 from jax.sharding import PartitionSpec as P
 
 
-SIZES = (256, 640, 128)
+SIZES = (384, 512, 128)
 UP_ROWS = (1536, 256, 128, 128)
 BLOCK = 256
+ROW = 4
+DETOUR = 416
 MIB = 1024 * 1024
 
 
@@ -34,8 +36,16 @@
     return first, value, second
 
 
-def mix_three(lower, own, upper):
-    total = lower.astype(jnp.float32) + own.astype(jnp.float32) + upper.astype(jnp.float32)
+def over_cycle(value, moves):
+    count = lax.axis_size("gossip")
+    pairs = [
+        (s, (s + moves[s % ROW]) % count) for s in range(count) if s % ROW in moves
+    ]
+    return lax.ppermute(value, "gossip", pairs)
+
+
+def mix_three(*parts):
+    total = sum(part.astype(jnp.float32) for part in parts)
     return (total / 3.0).astype(jnp.bfloat16)
 
 
@@ -47,6 +57,7 @@
         rest[-1][...] = mix_three(lower[...], own[...], upper[...])
 
     piece = pl.BlockSpec((block, width), lambda n: (n, 0))
+    aliased = before is not None and before.shape[0] == rows_out
     extra = [] if before is None else [before]
     return pl.pallas_call(
         body,
@@ -63,16 +74,24 @@
     return lax.dot_general(a, b, (dims, ((), ())), preferred_element_type=jnp.float32)
 
 
-def forward_body(core, *refs, in_scale):
-    tokens, w_gate, w_up, w_down = refs[:4]
-    outs = refs[4 : 8 + len(SIZES)]
-    (
-        tok, gate_v, up_v, down_t, hidden, hidden_t, slope, act, theirs, in_sems, out_sems,
-    ) = refs[8 + len(SIZES) :]
-    _, width = tok.shape
-    half = width // 2
-    blocks = hidden.shape[1] // BLOCK
-    at_theirs = pl.multiple_of((1 - core[0]) * half, half)
+def row_scale(tok):
+    wide = tok[...].astype(jnp.float32)
+    return lax.rsqrt(jnp.mean(wide * wide, axis=-1, keepdims=True) + 1e-06)
+
+
+def gate_and_up(tok, gate, up, scale):
+    gate_pre = jnp.dot(tok[...], gate, preferred_element_type=jnp.float32) * scale
+    up_pre = jnp.dot(tok[...], up, preferred_element_type=jnp.float32) * scale
+    return gate_pre, jax.nn.sigmoid(gate_pre), up_pre
+
+
+def forward_body(
+    core, tokens, w_gate, w_up, w_down, hidden_out, *refs, in_scale
+):
+    theirs_out = refs[: len(SIZES)]
+    tok, gate_v, up_v, down_t, hidden, theirs, in_sems, out_sems = refs[len(SIZES) :]
+    width = tok.shape[1]
+    blocks = gate_v.shape[1] // BLOCK
     done = []
 
     def fetch(n, src, dst):
@@ -94,7 +113,9 @@
         )
         for n in range(blocks)
     ]
-    copy_t = fetch(1 + 2 * blocks, w_down.at[:, pl.ds(at_theirs, half)], down_t)
+    at_theirs = pl.multiple_of((1 - core[0]) * (width // 2), width // 2)
+    down_part = w_down.at[:, pl.ds(at_theirs, down_t.shape[1])]
+    copy_t = fetch(1 + 2 * blocks, down_part, down_t)
     for copy in (tok_copy, *weight_copies[0]):
         copy.start()
     tok_copy.wait()
@@ -109,26 +130,11 @@
         for copy in weight_copies[n]:
             copy.wait()
         if n == 0:
-            wide = tok[...].astype(jnp.float32)
-            scale = lax.rsqrt(jnp.mean(wide * wide, axis=-1, keepdims=True) + 1e-06)
+            scale = row_scale(tok)
         cols = span(n)
-        gate_pre = jnp.dot(tok[...], gate_v[:, cols], preferred_element_type=jnp.float32)
-        up_pre = jnp.dot(tok[...], up_v[:, cols], preferred_element_type=jnp.float32)
-        gate_pre = gate_pre * (scale * in_scale)
-        up_pre = up_pre * (scale * in_scale)
-        sig = jax.nn.sigmoid(gate_pre)
-        activated = gate_pre * sig
-        value = (activated * up_pre).astype(jnp.bfloat16)
-        hidden[:, cols] = value
-        hidden_t[cols] = value.T
-        act[:, cols] = (activated * scale).astype(jnp.bfloat16)
-        slope[:, cols] = (up_pre * (sig * (1.0 + gate_pre * (1.0 - sig))) * scale).astype(
-            jnp.bfloat16
-        )
-        put(hidden.at[:, cols], outs[0].at[:, cols])
-        put(hidden_t.at[cols], outs[1].at[cols])
-        put(slope.at[:, cols], outs[2].at[:, cols])
-        put(act.at[:, cols], outs[3].at[:, cols])
+        gate_pre, sig, up_pre = gate_and_up(tok, gate_v[:, cols], up_v[:, cols], scale * in_scale)
+        hidden[:, cols] = (gate_pre * sig * up_pre).astype(jnp.bfloat16)
+        put(hidden.at[:, cols], hidden_out.at[:, cols])
     copy_t.wait()
     at = 0
     for n, size in enumerate(SIZES):
@@ -136,7 +142,7 @@
         theirs[:, cols] = jnp.dot(
             hidden[...], down_t[:, cols], preferred_element_type=jnp.float32
         ).astype(jnp.bfloat16)
-        put(theirs.at[:, cols], outs[4 + n])
+        put(theirs.at[:, cols], theirs_out[n])
         at += size
     for copy in done:
         copy.wait()
@@ -145,32 +151,67 @@
 def forward(core, tokens, w_gate, w_up, w_down, in_scale):
     rows, width = tokens.shape
     count = w_gate.shape[1]
-    half = width // 2
     anywhere = pl.BlockSpec(memory_space=pl.ANY)
-    shapes = [(rows, count), (count, rows), (rows, count), (rows, count)]
-    outs = [
-        jax.ShapeDtypeStruct(shape, jnp.bfloat16)
-        for shape in shapes + [(rows, size) for size in SIZES]
-    ]
+    shapes = [(rows, count)] + [(rows, size) for size in SIZES]
     blocks = count // BLOCK
     return pl.pallas_call(
         lambda *refs: forward_body(*refs, in_scale=in_scale),
         name="forward",
         in_specs=[pl.BlockSpec(memory_space=pltpu.SMEM)] + [anywhere] * 4,
-        out_specs=[anywhere] * len(outs),
-        out_shape=outs,
+        out_specs=[anywhere] * len(shapes),
+        out_shape=[jax.ShapeDtypeStruct(shape, jnp.bfloat16) for shape in shapes],
         scratch_shapes=[
             pltpu.VMEM((rows, width), jnp.bfloat16),
             pltpu.VMEM((width, count), jnp.bfloat16),
             pltpu.VMEM((width, count), jnp.bfloat16),
-            pltpu.VMEM((count, half), jnp.bfloat16),
-            *[pltpu.VMEM(shape, jnp.bfloat16) for shape in shapes],
-            pltpu.VMEM((rows, half), jnp.bfloat16),
+            pltpu.VMEM((count, width // 2), jnp.bfloat16),
+            pltpu.VMEM((rows, count), jnp.bfloat16),
+            pltpu.VMEM((rows, width // 2), jnp.bfloat16),
             pltpu.SemaphoreType.DMA((2 + 2 * blocks,)),
-            pltpu.SemaphoreType.DMA((4 * blocks + len(SIZES),)),
+            pltpu.SemaphoreType.DMA((len(SIZES) + blocks,)),
         ],
         compiler_params=pltpu.CompilerParams(vmem_limit_bytes=58 * MIB),
     )(core[None].astype(jnp.int32), tokens, w_gate, w_up, w_down)
+
+
+def slopes(tokens, w_gate, w_up, in_scale):
+    rows, width = tokens.shape
+    count = w_gate.shape[1]
+
+    def body(tok, w_gate, w_up, slope, act):
+        scale = row_scale(tok)
+        gate_pre, sig, up_pre = gate_and_up(tok, w_gate[...], w_up[...], scale * in_scale)
+        act[...] = (gate_pre * sig * scale).astype(jnp.bfloat16)
+        slope[...] = (up_pre * (sig * (1.0 + gate_pre * (1.0 - sig))) * scale).astype(jnp.bfloat16)
+
+    weights = pl.BlockSpec((width, BLOCK), lambda n: (0, n))
+    across = pl.BlockSpec((rows, BLOCK), lambda n: (0, n))
+    return pl.pallas_call(
+        body,
+        name="slopes",
+        grid=(count // BLOCK,),
+        in_specs=[pl.BlockSpec((rows, width), lambda n: (0, 0)), weights, weights],
+        out_specs=[across, across],
+        out_shape=[jax.ShapeDtypeStruct((rows, count), jnp.bfloat16)] * 2,
+        compiler_params=pltpu.CompilerParams(vmem_limit_bytes=40 * MIB),
+    )(tokens, w_gate, w_up)
+
+
+def turned(value):
+    rows, width = value.shape
+
+    def body(value, out):
+        out[...] = value[...].T
+
+    return pl.pallas_call(
+        body,
+        name="turned",
+        grid=(width // BLOCK,),
+        in_specs=[pl.BlockSpec((rows, BLOCK), lambda n: (0, n))],
+        out_specs=pl.BlockSpec((BLOCK, rows), lambda n: (n, 0)),
+        out_shape=jax.ShapeDtypeStruct((width, rows), value.dtype),
+        compiler_params=pltpu.CompilerParams(vmem_limit_bytes=4 * MIB),
+    )(value)
 
 
 def compute(tokens, targets, gate_weight, up_weight, down_weight):
@@ -190,9 +231,9 @@
     mine = core * half
     theirs = half - mine
 
-    outs = forward(core, inputs, w_gate, w_up, w_down, in_scale)
-    hidden, hidden_t, slope_gate, act = outs[:4]
-    sums_theirs = outs[4:]
+    hidden, *sums_theirs = forward(core, inputs, w_gate, w_up, w_down, in_scale)
+    slope_gate, act = slopes(inputs, w_gate, w_up, in_scale)
+    hidden_t = turned(hidden)
 
     def columns(array, start, size):
         return lax.dynamic_slice_in_dim(array, start, size, 1)
@@ -200,8 +241,10 @@
     def stepped_down(err, start):
         grad = dot(hidden_t, err, ((1,), (0,))) * mid_scale
         w_piece = columns(w_down, start, err.shape[1])
-        new = (w_piece.astype(jnp.float32) - step_size * grad).astype(jnp.bfloat16)
-        down_parts.append((start, both_ways(new)))
+        return (w_piece.astype(jnp.float32) - step_size * grad).astype(jnp.bfloat16)
+
+    def send_down(err, start):
+        down_parts.append((start, both_ways(stepped_down(err, start))))
 
     totals = []
     far = []
@@ -228,10 +271,21 @@
         err = ((offset + output) / tok_count).astype(jnp.bfloat16)
         err_mine.append(err)
         err_theirs.append(other_core(err))
-        stepped_down(err, mine + at)
+        if n:
+            send_down(err, mine + at)
+        else:
+            new = stepped_down(err, mine)
+            even = exchange(new, 0)
+            inside = over_cycle(new, {1: 1, 2: -1})
+            relay = over_cycle(new[:DETOUR], {3: -1, 0: 1})
+            crossed = over_cycle(new[DETOUR:], {3: 1, 0: -1})
+            relay = over_cycle(relay, {2: ROW, 1: -ROW})
+            relay = over_cycle(relay, {2: -1, 1: 1})
+            relay = over_cycle(relay, {1: -1, 2: 1})
+            down_parts.append((mine, (new, even, inside, (relay, crossed))))
         at += size
     err_t = jnp.concatenate(err_theirs, 1)
-    stepped_down(err_t, theirs)
+    send_down(err_t, theirs)
 
     grad_hidden = dot(
         jnp.concatenate(err_mine, 1), columns(w_down, mine, half), ((1,), (1,))
@@ -255,8 +309,16 @@
         row += rows
 
     down_out = jnp.zeros_like(w_down)
-    for start, parts in down_parts:
-        down_out = lax.dynamic_update_slice(down_out, mix_three(*parts), (0, start))
+    for n, (start, parts) in enumerate(down_parts):
+        if n == 0:
+            row = 0
+            for part in parts[3]:
+                rows = slice(row, row + part.shape[0])
+                mixed = mix_three(*(whole[rows] for whole in parts[:3]), part)
+                down_out = lax.dynamic_update_slice(down_out, mixed, (row, start))
+                row += part.shape[0]
+        else:
+            down_out = lax.dynamic_update_slice(down_out, mix_three(*parts), (0, start))
     gate_out = mix_rows(None, width, 0, gate_parts)
     up_out = gate_out[:16]
     for start, parts in up_parts:

time: 359 us -> 432 us (1.20)
  starting transfers between devices: 49.2 us -> 87.3 us
  waiting for transfers between devices: 234 us -> 256 us
  Pallas kernels: 30.7 us -> 37.5 us
    ppermute x18 -> x17, starting transfers between devices: 40.6 us -> 65.9 us  [exchange(): return lax.ppermute(value, 'gossip', pairs)]
    ppermute x0 -> x6, waiting for transfers between devices: none -> 15.2 us  [over_cycle(): return lax.ppermute(value, 'gossip', pairs)]
    ppermute x0 -> x6, starting transfers between devices: none -> 13.2 us  [over_cycle(): return lax.ppermute(value, 'gossip', pairs)]
    pallas_call x0 -> x2, Pallas kernels: none -> 7.67 us  [the longest x1 7 us: slopes(): pl.pallas_call(body, name='slopes', grid=(count // BLOCK,), in_specs=[pl....]
    ppermute x18 -> x17, waiting for transfers between devices: 220 us -> 227 us  [exchange(): return lax.ppermute(value, 'gossip', pairs)]
    unnamed x66 -> x74, local copies, waits for them, and re-layouts: 6.67 us -> 9.95 us
  transfers between devices with their start and end apart: 27 -> 32, of which waited for: 4 -> 7; matrix products, arithmetic and copies ran while one was open for 10% -> 9% of each run, Pallas kernels for 5% -> 6%
where the time goes in v3:
time: 432 us; the launch traced here: 431 us
  waiting for transfers between devices  256 us (59%)
  starting transfers between devices  87.3 us (20%)
  Pallas kernels  37.5 us (9%)
  matrix products  23 us (5%)
  other arithmetic  14.1 us (3%)
  local copies, waits for them, and re-layouts  12 us (3%)
    ppermute x17, waiting for transfers between devices, exchange(): return lax.ppermute(value, 'gossip', pairs)  227 us
    ppermute x17, starting transfers between devices, exchange(): return lax.ppermute(value, 'gossip', pairs)  65.9 us
    dot_general x14, matrix products, dot(): lax.dot_general(a, b, (dims, ((), ())), preferred_element_type=jnp.float32)  23 us
    pallas_call x5, Pallas kernels, mix_rows(): pl.pallas_call(body, grid=(rows // block,), in_specs=[piece] * 3 + [pl.Bl...  19.6 us
    ppermute x6, waiting for transfers between devices, over_cycle(): return lax.ppermute(value, 'gossip', pairs)  15.2 us
    ppermute x6, starting transfers between devices, over_cycle(): return lax.ppermute(value, 'gossip', pairs)  13.2 us
    ppermute x3, waiting for transfers between devices, other_chip(): return lax.ppermute(value, 'mp', [(s, s ^ 2) for s in range(count)])  12.4 us
    pallas_call x1, Pallas kernels, forward(): pl.pallas_call(lambda *refs: forward_body(*refs, in_scale=in_scale), name...  10.2 us
  transfers between devices with their start and end apart: 32, of which 7 were waited for; matrix products, arithmetic and copies ran while one was open for 9% of the time, Pallas kernels for 6%

profile of v3, /device:TPU:0, one launch (start us, length us, event | category | flops | bytes accessed | tf_op | source)
XLA Modules:
  0.0 430.8 jit_solution(10468074264047101717)
XLA Ops:
  0.6 10.2 %forward.1 = (bf16[512,1024]{1,0:T(8,128)(2,1)}, bf16[512,384]{1,0:T(8,128)(2,1)}, bf16[512,512]{1,0:T(8,128)(2,1)}, bf16[512,128]{1,0:T(8,128)(2,1)}) custom-call(s32[1]{0:T(128)} %bitcast.2.refs_0_, bf16[512,2048]{1,0:T(8,128)(2,1)} %bitcast.127, bf16[2048,1024]{1,0:T(8,128)(2,1)} %bitcast.123, bf16[2048,1024]{1,0:T(8,128)(2,1)} %bitcast.125, ...), custom_call_target="tpu_custom_call" | custom-call | tf_op jit(solution)/shard_map/forward/pallas_call | solution.py:157
  11.5 3.2 fusion.31
  17.0 3.3 collective-permute-start.5
  29.1 7.0 %slopes.1 = (bf16[512,1024]{1,0:T(8,128)(2,1)S(1)}, bf16[512,1024]{1,0:T(8,128)(2,1)S(1)}) custom-call(bf16[512,2048]{1,0:T(8,128)(2,1)S(1)} %bitcast.128, bf16[2048,1024]{1,0:T(8,128)(2,1)S(1)} %bitcast.124, bf16[2048,1024]{1,0:T(8,128)(2,1)S(1)} %bitcast.126), custom_call_target="tpu_custom_call" | custom-call | tf_op jit(solution)/shard_map/slopes/pallas_call | solution.py:189
  42.5 7.3 %collective-permute-start.28 = (bf16[1024,128]{1,0:T(8,128)(2,1)S(1)}, bf16[1024,128]{1,0:T(8,128)(2,1)S(1)}, u32[]{:S(2)}, u32[]{:S(2)}) collective-permute-start(bf16[1024,128]{1,0:T(8,128)(2,1)S(1)} %fusion.21), channel_id=1, source_target_pairs={{0,124},{4,8},{8,4},{12,16},{16,12},{20,24},{24,20},{28,32},{32,28... | collective-permute-start | bytes 786440 | tf_op jit(solution)/shard_map/ppermute | solution.py:20
  51.0 3.1 collective-permute-start.3
  54.2 5.6 %collective-permute-done.1 = bf16[512,384]{1,0:T(8,128)(2,1)S(1)} collective-permute-done((bf16[512,384]{1,0:T(8,128)(2,1)S(1)}, bf16[512,384]{1,0:T(8,128)(2,1)S(1)}, u32[]{:S(2)}, u32[]{:S(2)}) %collective-permute-start.1) | collective-permute-done | bytes 393248 | tf_op jit(solution)/shard_map/ppermute | solution.py:30
  63.5 6.8 %collective-permute-done.3 = bf16[512,512]{1,0:T(8,128)(2,1)S(1)} collective-permute-done((bf16[512,512]{1,0:T(8,128)(2,1)S(1)}, bf16[512,512]{1,0:T(8,128)(2,1)S(1)}, u32[]{:S(2)}, u32[]{:S(2)}) %collective-permute-start.3) | collective-permute-done | bytes 524320 | tf_op jit(solution)/shard_map/ppermute | solution.py:30
  76.5 8.2 %collective-permute-start.25 = (bf16[608,384]{1,0:T(8,128)(2,1)S(1)}, bf16[608,384]{1,0:T(8,128)(2,1)S(1)}, u32[]{:S(2)}, u32[]{:S(2)}) collective-permute-start(bf16[608,384]{1,0:T(8,128)(2,1)S(1)} %slice.74), channel_id=1, source_target_pairs={{0,124},{12,16},{16,12},{28,32},{32,28},{44,48},{48,44},{60,64},{6... | collective-permute-start | bytes 1400840 | tf_op jit(solution)/shard_map/ppermute | solution.py:44
  90.1 5.9 %collective-permute-done.25 = bf16[608,384]{1,0:T(8,128)(2,1)S(1)} collective-permute-done((bf16[608,384]{1,0:T(8,128)(2,1)S(1)}, bf16[608,384]{1,0:T(8,128)(2,1)S(1)}, u32[]{:S(2)}, u32[]{:S(2)}) %collective-permute-start.25) | collective-permute-done | bytes 466976 | tf_op jit(solution)/shard_map/ppermute | solution.py:44
  97.6 5.0 %collective-permute-start.30 = (bf16[1024,1024]{1,0:T(8,128)(2,1)S(1)}, bf16[1024,1024]{1,0:T(8,128)(2,1)}, u32[]{:S(2)}, u32[]{:S(2)}) collective-permute-start(bf16[1024,1024]{1,0:T(8,128)(2,1)S(1)} %subtract_convert_fusion), channel_id=1, source_target_pairs={{0,124},{4,8},{8,4},{12,16},{16,12},{20,24},{24,20},{28,32},{32,28... | collective-permute-start | bytes 6291464 | tf_op jit(solution)/shard_map/ppermute | solution.py:20
  104.0 2.8 fusion.own
  106.8 13.0 %collective-permute-start.10 = (bf16[2048,1024]{1,0:T(8,128)(2,1)S(1)}, bf16[2048,1024]{1,0:T(8,128)(2,1)S(1)}, u32[]{:S(2)}, u32[]{:S(2)}) collective-permute-start(bf16[2048,1024]{1,0:T(8,128)(2,1)S(1)} %fusion.own), channel_id=1, source_target_pairs={{0,4},{4,0},{8,12},{12,8},{16,20},{20,16},{24,28},{28,24},{32,36},... | collective-permute-start | bytes 12582920 | tf_op jit(solution)/shard_map/ppermute | solution.py:20
  119.8 9.3 %collective-permute-done.24 = bf16[416,384]{1,0:T(8,128)(2,1)S(1)} collective-permute-done((bf16[416,384]{1,0:T(8,128)(2,1)S(1)}, bf16[416,384]{1,0:T(8,128)(2,1)S(1)}, u32[]{:S(2)}, u32[]{:S(2)}) %collective-permute-start.24) | collective-permute-done | bytes 319520 | tf_op jit(solution)/shard_map/ppermute | solution.py:44
  129.1 6.6 %collective-permute-start.9 = (bf16[2048,1024]{1,0:T(8,128)(2,1)S(1)}, bf16[2048,1024]{1,0:T(8,128)(2,1)S(1)}, u32[]{:S(2)}, u32[]{:S(2)}) collective-permute-start(bf16[2048,1024]{1,0:T(8,128)(2,1)S(1)} %fusion.own), channel_id=1, source_target_pairs={{0,124},{4,8},{8,4},{12,16},{16,12},{20,24},{24,20},{28,32},{32,28... | collective-permute-start | bytes 12582920 | tf_op jit(solution)/shard_map/ppermute | solution.py:20
  136.5 3.6 fusion.1.own
  140.2 6.0 %collective-permute-start.17 = (bf16[1536,1024]{1,0:T(8,128)(2,1)S(1)}, bf16[1536,1024]{1,0:T(8,128)(2,1)S(1)}, u32[]{:S(2)}, u32[]{:S(2)}) collective-permute-start(bf16[1536,1024]{1,0:T(8,128)(2,1)S(1)} %fusion.1.own), channel_id=1, source_target_pairs={{0,124},{4,8},{8,4},{12,16},{16,12},{20,24},{24,20},{28,32},{32,28... | collective-permute-start | bytes 9437192 | tf_op jit(solution)/shard_map/ppermute | solution.py:20
  146.1 120.5 %collective-permute-done.15.lower = bf16[256,1024]{1,0:T(8,128)(2,1)S(1)} collective-permute-done((bf16[256,1024]{1,0:T(8,128)(2,1)S(1)}, bf16[256,1024]{1,0:T(8,128)(2,1)S(1)}, u32[]{:S(2)}, u32[]{:S(2)}) %collective-permute-start.15) | collective-permute-done | bytes 524320 | tf_op jit(solution)/shard_map/ppermute | solution.py:20
  266.6 17.5 %collective-permute-start.18 = (bf16[1536,1024]{1,0:T(8,128)(2,1)S(1)}, bf16[1536,1024]{1,0:T(8,128)(2,1)S(1)}, u32[]{:S(2)}, u32[]{:S(2)}) collective-permute-start(bf16[1536,1024]{1,0:T(8,128)(2,1)S(1)} %fusion.1.own), channel_id=1, source_target_pairs={{0,4},{4,0},{8,12},{12,8},{16,20},{20,16},{24,28},{28,24},{32,36},... | collective-permute-start | bytes 9437192 | tf_op jit(solution)/shard_map/ppermute | solution.py:20
  288.5 106.7 %collective-permute-done.31 = bf16[1024,1024]{1,0:T(8,128)(2,1)} collective-permute-done((bf16[1024,1024]{1,0:T(8,128)(2,1)S(1)}, bf16[1024,1024]{1,0:T(8,128)(2,1)}, u32[]{:S(2)}, u32[]{:S(2)}) %collective-permute-start.31) | collective-permute-done | bytes 2097184 | tf_op jit(solution)/shard_map/ppermute | solution.py:20
  399.7 4.1 collective-permute-start.11
  405.9 3.8 fusion.3
  409.7 10.1 %shard_map.76 = bf16[2048,1024]{1,0:T(8,128)(2,1)} custom-call(bf16[2048,1024]{1,0:T(8,128)(2,1)} %copy-done.18, bf16[2048,1024]{1,0:T(8,128)(2,1)} %copy-done.16, bf16[2048,1024]{1,0:T(8,128)(2,1)} %copy-done.17), custom_call_target="tpu_custom_call" | custom-call | tf_op jit(solution)/shard_map/pallas_call | solution.py:62
  421.2 6.9 %shard_map.77.rest_0_ = bf16[2048,1024]{1,0:T(8,128)(2,1)} custom-call(bf16[1536,1024]{1,0:T(8,128)(2,1)} %copy-done.20, bf16[1536,1024]{1,0:T(8,128)(2,1)} %copy-done.19, bf16[1536,1024]{1,0:T(8,128)(2,1)} %copy-done.21, bf16[16,1024]{1,0:T(8,128)(2,1)} %slice.70.rest_0_), custom_call_target="tpu_custom_call" | custom-call | tf_op jit(solution)/shard_map/pallas_call | solution.py:62
  (152 shorter events, 52.9 us)
Async XLA Ops:
  10.9 28.4 %collective-permute-start = (bf16[512,384]{1,0:T(8,128)(2,1)}, bf16[512,384]{1,0:T(8,128)(2,1)}, u32[]{:S(2)}, u32[]{:S(2)}) collective-permute-start(bf16[512,384]{1,0:T(8,128)(2,1)} %get-tuple-element.10), channel_id=1, source_target_pairs={{0,1},{1,0},{2,3},{3,2},{4,5},{5,4},{6,7},{7,6},{8,9},{9,8},{10,11... | collective-permute-start | bytes 1179656 | tf_op jit(solution)/shard_map/ppermute | solution.py:25
  11.0 38.8 %collective-permute-start.2 = (bf16[512,512]{1,0:T(8,128)(2,1)}, bf16[512,512]{1,0:T(8,128)(2,1)}, u32[]{:S(2)}, u32[]{:S(2)}) collective-permute-start(bf16[512,512]{1,0:T(8,128)(2,1)} %get-tuple-element.11), channel_id=1, source_target_pairs={{0,1},{1,0},{2,3},{3,2},{4,5},{5,4},{6,7},{7,6},{8,9},{9,8},{10,11... | collective-permute-start | bytes 1572872 | tf_op jit(solution)/shard_map/ppermute | solution.py:25
  17.0 21.1 %collective-permute-start.5 = (bf16[512,128]{1,0:T(8,128)(2,1)}, bf16[512,128]{1,0:T(8,128)(2,1)}, u32[]{:S(2)}, u32[]{:S(2)}) collective-permute-start(bf16[512,128]{1,0:T(8,128)(2,1)} %fusion.55), channel_id=1, source_target_pairs={{0,2},{1,3},{2,0},{3,1},{4,6},{5,7},{6,4},{7,5},{8,10},{9,11},{10,... | collective-permute-start | bytes 393224 | tf_op jit(solution)/shard_map/ppermute | solution.py:30
  42.5 44.5 %collective-permute-start.28 = (bf16[1024,128]{1,0:T(8,128)(2,1)S(1)}, bf16[1024,128]{1,0:T(8,128)(2,1)S(1)}, u32[]{:S(2)}, u32[]{:S(2)}) collective-permute-start(bf16[1024,128]{1,0:T(8,128)(2,1)S(1)} %fusion.21), channel_id=1, source_target_pairs={{0,124},{4,8},{8,4},{12,16},{16,12},{20,24},{24,20},{28,32},{32,28... | collective-permute-start | bytes 786440 | tf_op jit(solution)/shard_map/ppermute | solution.py:20
  49.8 40.2 %collective-permute-start.29 = (bf16[1024,128]{1,0:T(8,128)(2,1)S(1)}, bf16[1024,128]{1,0:T(8,128)(2,1)S(1)}, u32[]{:S(2)}, u32[]{:S(2)}) collective-permute-start(bf16[1024,128]{1,0:T(8,128)(2,1)S(1)} %fusion.21), channel_id=1, source_target_pairs={{0,4},{4,0},{8,12},{12,8},{16,20},{20,16},{24,28},{28,24},{32,36},... | collective-permute-start | bytes 786440 | tf_op jit(solution)/shard_map/ppermute | solution.py:20
  62.1 22.6 %collective-permute-start.21 = (bf16[416,384]{1,0:T(8,128)(2,1)S(1)}, bf16[416,384]{1,0:T(8,128)(2,1)S(1)}, u32[]{:S(2)}, u32[]{:S(2)}) collective-permute-start(bf16[416,384]{1,0:T(8,128)(2,1)S(1)} %slice.71), channel_id=1, source_target_pairs={{0,4},{12,8},{16,20},{28,24},{32,36},{44,40},{48,52},{60,56},{64,6... | collective-permute-start | bytes 958472 | tf_op jit(solution)/shard_map/ppermute | solution.py:44
  75.6 22.0 %collective-permute-start.19 = (bf16[1024,384]{1,0:T(8,128)(2,1)S(1)}, bf16[1024,384]{1,0:T(8,128)(2,1)S(1)}, u32[]{:S(2)}, u32[]{:S(2)}) collective-permute-start(bf16[1024,384]{1,0:T(8,128)(2,1)S(1)} %subtract_convert_fusion.2), channel_id=1, source_target_pairs={{0,4},{4,0},{8,12},{12,8},{16,20},{20,16},{24,28},{28,24},{32,36},... | collective-permute-start | bytes 2359304 | tf_op jit(solution)/shard_map/ppermute | solution.py:20
  76.5 19.4 %collective-permute-start.25 = (bf16[608,384]{1,0:T(8,128)(2,1)S(1)}, bf16[608,384]{1,0:T(8,128)(2,1)S(1)}, u32[]{:S(2)}, u32[]{:S(2)}) collective-permute-start(bf16[608,384]{1,0:T(8,128)(2,1)S(1)} %slice.74), channel_id=1, source_target_pairs={{0,124},{12,16},{16,12},{28,32},{32,28},{44,48},{48,44},{60,64},{6... | collective-permute-start | bytes 1400840 | tf_op jit(solution)/shard_map/ppermute | solution.py:44
  87.0 19.8 %collective-permute-start.20 = (bf16[1024,384]{1,0:T(8,128)(2,1)S(1)}, bf16[1024,384]{1,0:T(8,128)(2,1)S(1)}, u32[]{:S(2)}, u32[]{:S(2)}) collective-permute-start(bf16[1024,384]{1,0:T(8,128)(2,1)S(1)} %subtract_convert_fusion.2), channel_id=1, source_target_pairs={{4,8},{8,4},{20,24},{24,20},{36,40},{40,36},{52,56},{56,52},{68,72... | collective-permute-start | bytes 2359304 | tf_op jit(solution)/shard_map/ppermute | solution.py:44
  90.0 46.2 %collective-permute-start.26 = (bf16[1024,512]{1,0:T(8,128)(2,1)}, bf16[1024,512]{1,0:T(8,128)(2,1)S(1)}, u32[]{:S(2)}, u32[]{:S(2)}) collective-permute-start(bf16[1024,512]{1,0:T(8,128)(2,1)} %subtract_convert_fusion.1), channel_id=1, source_target_pairs={{0,124},{4,8},{8,4},{12,16},{16,12},{20,24},{24,20},{28,32},{32,28... | collective-permute-start | bytes 3145736 | tf_op jit(solution)/shard_map/ppermute | solution.py:20
  96.0 44.2 %collective-permute-start.27 = (bf16[1024,512]{1,0:T(8,128)(2,1)}, bf16[1024,512]{1,0:T(8,128)(2,1)}, u32[]{:S(2)}, u32[]{:S(2)}) collective-permute-start(bf16[1024,512]{1,0:T(8,128)(2,1)} %subtract_convert_fusion.1), channel_id=1, source_target_pairs={{0,4},{4,0},{8,12},{12,8},{16,20},{20,16},{24,28},{28,24},{32,36},... | collective-permute-start | bytes 3145736 | tf_op jit(solution)/shard_map/ppermute | solution.py:20
  97.6 186.4 %collective-permute-start.30 = (bf16[1024,1024]{1,0:T(8,128)(2,1)S(1)}, bf16[1024,1024]{1,0:T(8,128)(2,1)}, u32[]{:S(2)}, u32[]{:S(2)}) collective-permute-start(bf16[1024,1024]{1,0:T(8,128)(2,1)S(1)} %subtract_convert_fusion), channel_id=1, source_target_pairs={{0,124},{4,8},{8,4},{12,16},{16,12},{20,24},{24,20},{28,32},{32,28... | collective-permute-start | bytes 6291464 | tf_op jit(solution)/shard_map/ppermute | solution.py:20
  102.6 26.4 %collective-permute-start.24 = (bf16[416,384]{1,0:T(8,128)(2,1)S(1)}, bf16[416,384]{1,0:T(8,128)(2,1)S(1)}, u32[]{:S(2)}, u32[]{:S(2)}) collective-permute-start(bf16[416,384]{1,0:T(8,128)(2,1)S(1)} %collective-permute-done.23), channel_id=1, source_target_pairs={{4,0},{8,12},{20,16},{24,28},{36,32},{40,44},{52,48},{56,60},{68,6... | collective-permute-start | bytes 958472 | tf_op jit(solution)/shard_map/ppermute | solution.py:44
  106.8 292.9 %collective-permute-start.10 = (bf16[2048,1024]{1,0:T(8,128)(2,1)S(1)}, bf16[2048,1024]{1,0:T(8,128)(2,1)S(1)}, u32[]{:S(2)}, u32[]{:S(2)}) collective-permute-start(bf16[2048,1024]{1,0:T(8,128)(2,1)S(1)} %fusion.own), channel_id=1, source_target_pairs={{0,4},{4,0},{8,12},{12,8},{16,20},{20,16},{24,28},{28,24},{32,36},... | collective-permute-start | bytes 12582920 | tf_op jit(solution)/shard_map/ppermute | solution.py:20
  129.1 274.8 %collective-permute-start.9 = (bf16[2048,1024]{1,0:T(8,128)(2,1)S(1)}, bf16[2048,1024]{1,0:T(8,128)(2,1)S(1)}, u32[]{:S(2)}, u32[]{:S(2)}) collective-permute-start(bf16[2048,1024]{1,0:T(8,128)(2,1)S(1)} %fusion.own), channel_id=1, source_target_pairs={{0,124},{4,8},{8,4},{12,16},{16,12},{20,24},{24,20},{28,32},{32,28... | collective-permute-start | bytes 12582920 | tf_op jit(solution)/shard_map/ppermute | solution.py:20
  136.2 130.4 %collective-permute-start.15 = (bf16[256,1024]{1,0:T(8,128)(2,1)S(1)}, bf16[256,1024]{1,0:T(8,128)(2,1)S(1)}, u32[]{:S(2)}, u32[]{:S(2)}) collective-permute-start(bf16[256,1024]{1,0:T(8,128)(2,1)S(1)} %fusion.15.own), channel_id=1, source_target_pairs={{0,124},{4,8},{8,4},{12,16},{16,12},{20,24},{24,20},{28,32},{32,28... | collective-permute-start | bytes 1572872 | tf_op jit(solution)/shard_map/ppermute | solution.py:20
  140.2 257.3 %collective-permute-start.17 = (bf16[1536,1024]{1,0:T(8,128)(2,1)S(1)}, bf16[1536,1024]{1,0:T(8,128)(2,1)S(1)}, u32[]{:S(2)}, u32[]{:S(2)}) collective-permute-start(bf16[1536,1024]{1,0:T(8,128)(2,1)S(1)} %fusion.1.own), channel_id=1, source_target_pairs={{0,124},{4,8},{8,4},{12,16},{16,12},{20,24},{24,20},{28,32},{32,28... | collective-permute-start | bytes 9437192 | tf_op jit(solution)/shard_map/ppermute | solution.py:20
  266.6 133.1 %collective-permute-start.18 = (bf16[1536,1024]{1,0:T(8,128)(2,1)S(1)}, bf16[1536,1024]{1,0:T(8,128)(2,1)S(1)}, u32[]{:S(2)}, u32[]{:S(2)}) collective-permute-start(bf16[1536,1024]{1,0:T(8,128)(2,1)S(1)} %fusion.1.own), channel_id=1, source_target_pairs={{0,4},{4,0},{8,12},{12,8},{16,20},{20,16},{24,28},{28,24},{32,36},... | collective-permute-start | bytes 9437192 | tf_op jit(solution)/shard_map/ppermute | solution.py:20
  284.0 111.2 %collective-permute-start.31 = (bf16[1024,1024]{1,0:T(8,128)(2,1)S(1)}, bf16[1024,1024]{1,0:T(8,128)(2,1)}, u32[]{:S(2)}, u32[]{:S(2)}) collective-permute-start(bf16[1024,1024]{1,0:T(8,128)(2,1)S(1)} %subtract_convert_fusion), channel_id=1, source_target_pairs={{0,4},{4,0},{8,12},{12,8},{16,20},{20,16},{24,28},{28,24},{32,36},... | collective-permute-start | bytes 6291464 | tf_op jit(solution)/shard_map/ppermute | solution.py:20
  395.2 32.9 %collective-permute-start.16 = (bf16[256,1024]{1,0:T(8,128)(2,1)S(1)}, bf16[256,1024]{1,0:T(8,128)(2,1)S(1)}, u32[]{:S(2)}, u32[]{:S(2)}) collective-permute-start(bf16[256,1024]{1,0:T(8,128)(2,1)S(1)} %fusion.15.own), channel_id=1, source_target_pairs={{0,4},{4,0},{8,12},{12,8},{16,20},{20,16},{24,28},{28,24},{32,36},... | collective-permute-start | bytes 1572872 | tf_op jit(solution)/shard_map/ppermute | solution.py:20
  397.4 31.7 %collective-permute-start.13 = (bf16[128,1024]{1,0:T(8,128)(2,1)S(1)}, bf16[128,1024]{1,0:T(8,128)(2,1)S(1)}, u32[]{:S(2)}, u32[]{:S(2)}) collective-permute-start(bf16[128,1024]{1,0:T(8,128)(2,1)S(1)} %fusion.22.own), channel_id=1, source_target_pairs={{0,124},{4,8},{8,4},{12,16},{16,12},{20,24},{24,20},{28,32},{32,28... | collective-permute-start | bytes 786440 | tf_op jit(solution)/shard_map/ppermute | solution.py:20
  399.7 29.4 %collective-permute-start.14 = (bf16[128,1024]{1,0:T(8,128)(2,1)S(1)}, bf16[128,1024]{1,0:T(8,128)(2,1)S(1)}, u32[]{:S(2)}, u32[]{:S(2)}) collective-permute-start(bf16[128,1024]{1,0:T(8,128)(2,1)S(1)} %fusion.22.own), channel_id=1, source_target_pairs={{0,4},{4,0},{8,12},{12,8},{16,20},{20,16},{24,28},{28,24},{32,36},... | collective-permute-start | bytes 786440 | tf_op jit(solution)/shard_map/ppermute | solution.py:20
  399.7 30.2 %collective-permute-start.11 = (bf16[128,1024]{1,0:T(8,128)(2,1)S(1)}, bf16[128,1024]{1,0:T(8,128)(2,1)S(1)}, u32[]{:S(2)}, u32[]{:S(2)}) collective-permute-start(bf16[128,1024]{1,0:T(8,128)(2,1)S(1)} %fusion.23.own), channel_id=1, source_target_pairs={{0,124},{4,8},{8,4},{12,16},{16,12},{20,24},{24,20},{28,32},{32,28... | collective-permute-start | bytes 786440 | tf_op jit(solution)/shard_map/ppermute | solution.py:20
  403.9 26.0 %collective-permute-start.12 = (bf16[128,1024]{1,0:T(8,128)(2,1)S(1)}, bf16[128,1024]{1,0:T(8,128)(2,1)S(1)}, u32[]{:S(2)}, u32[]{:S(2)}) collective-permute-start(bf16[128,1024]{1,0:T(8,128)(2,1)S(1)} %fusion.23.own), channel_id=1, source_target_pairs={{0,4},{4,0},{8,12},{12,8},{16,20},{20,16},{24,28},{28,24},{32,36},... | collective-permute-start | bytes 786440 | tf_op jit(solution)/shard_map/ppermute | solution.py:20
  (44 other events, 922.1 us)

commit v4 on v3

--- a/solution.py
+++ b/solution.py
@@ -7,10 +7,10 @@
 
 
 SIZES = (384, 512, 128)
-UP_ROWS = (1536, 256, 128, 128)
+UP_ROWS = (1792, 128, 64, 64)
 BLOCK = 256
 ROW = 4
-DETOUR = 416
+DETOUR = 400
 MIB = 1024 * 1024
 
 
@@ -86,10 +86,9 @@
 
 
 def forward_body(
-    core, tokens, w_gate, w_up, w_down, hidden_out, *refs, in_scale
+    core, tokens, w_gate, w_up, w_down, hidden_out, theirs_out,
+    tok, gate_v, up_v, down_t, hidden, theirs, in_sems, out_sems, *, in_scale
 ):
-    theirs_out = refs[: len(SIZES)]
-    tok, gate_v, up_v, down_t, hidden, theirs, in_sems, out_sems = refs[len(SIZES) :]
     width = tok.shape[1]
     blocks = gate_v.shape[1] // BLOCK
     done = []
@@ -136,14 +135,10 @@
         hidden[:, cols] = (gate_pre * sig * up_pre).astype(jnp.bfloat16)
         put(hidden.at[:, cols], hidden_out.at[:, cols])
     copy_t.wait()
-    at = 0
-    for n, size in enumerate(SIZES):
-        cols = slice(at, at + size)
-        theirs[:, cols] = jnp.dot(
-            hidden[...], down_t[:, cols], preferred_element_type=jnp.float32
-        ).astype(jnp.bfloat16)
-        put(theirs.at[:, cols], theirs_out[n])
-        at += size
+    theirs[...] = jnp.dot(hidden[...], down_t[...], preferred_element_type=jnp.float32).astype(
+        jnp.bfloat16
+    )
+    put(theirs, theirs_out)
     for copy in done:
         copy.wait()
 
@@ -152,7 +147,7 @@
     rows, width = tokens.shape
     count = w_gate.shape[1]
     anywhere = pl.BlockSpec(memory_space=pl.ANY)
-    shapes = [(rows, count)] + [(rows, size) for size in SIZES]
+    shapes = [(rows, count), (rows, SIZES[0])]
     blocks = count // BLOCK
     return pl.pallas_call(
         lambda *refs: forward_body(*refs, in_scale=in_scale),
@@ -164,11 +159,10 @@
             pltpu.VMEM((rows, width), jnp.bfloat16),
             pltpu.VMEM((width, count), jnp.bfloat16),
             pltpu.VMEM((width, count), jnp.bfloat16),
-            pltpu.VMEM((count, width // 2), jnp.bfloat16),
-            pltpu.VMEM((rows, count), jnp.bfloat16),
-            pltpu.VMEM((rows, width // 2), jnp.bfloat16),
+            pltpu.VMEM((count, SIZES[0]), jnp.bfloat16),
+            *[pltpu.VMEM(shape, jnp.bfloat16) for shape in shapes],
             pltpu.SemaphoreType.DMA((2 + 2 * blocks,)),
-            pltpu.SemaphoreType.DMA((len(SIZES) + blocks,)),
+            pltpu.SemaphoreType.DMA((1 + blocks,)),
         ],
         compiler_params=pltpu.CompilerParams(vmem_limit_bytes=58 * MIB),
     )(core[None].astype(jnp.int32), tokens, w_gate, w_up, w_down)
@@ -231,7 +225,7 @@
     mine = core * half
     theirs = half - mine
 
-    hidden, *sums_theirs = forward(core, inputs, w_gate, w_up, w_down, in_scale)
+    hidden, first_sent = forward(core, inputs, w_gate, w_up, w_down, in_scale)
     slope_gate, act = slopes(inputs, w_gate, w_up, in_scale)
     hidden_t = turned(hidden)
 
@@ -246,14 +240,22 @@
     def send_down(err, start):
         down_parts.append((start, both_ways(stepped_down(err, start))))
 
+    rest = half - SIZES[0]
+    rest_sent = dot(hidden, columns(w_down, theirs + SIZES[0], rest), ((1,), (0,)))
+    rest_sent = rest_sent.astype(jnp.bfloat16)
+    arrived = []
+    own = []
+    for sent, start, size in ((first_sent, 0, SIZES[0]), (rest_sent, SIZES[0], rest)):
+        arrived.append(other_core(sent))
+        value = dot(hidden, columns(w_down, mine + start, size), ((1,), (0,)))
+        own.append(lax.optimization_barrier(value))
     totals = []
     far = []
     at = 0
     for n, size in enumerate(SIZES):
-        arrived = other_core(sums_theirs[n])
-        own = dot(hidden, columns(w_down, mine + at, size), ((1,), (0,)))
-        own = lax.optimization_barrier(own)
-        total = own + arrived.astype(jnp.float32)
+        which = min(n, 1)
+        cols = slice(at - which * SIZES[0], at - which * SIZES[0] + size)
+        total = own[which][:, cols] + arrived[which][:, cols].astype(jnp.float32)
         rounded = total.astype(jnp.bfloat16)
         totals.append(total)
         far.append(other_chip(rounded))
@@ -277,8 +279,9 @@
             new = stepped_down(err, mine)
             even = exchange(new, 0)
             inside = over_cycle(new, {1: 1, 2: -1})
-            relay = over_cycle(new[:DETOUR], {3: -1, 0: 1})
-            crossed = over_cycle(new[DETOUR:], {3: 1, 0: -1})
+            relay, crossed = lax.optimization_barrier((new[:DETOUR], new[DETOUR:]))
+            relay = over_cycle(relay, {3: -1, 0: 1})
+            crossed = over_cycle(crossed, {3: 1, 0: -1})
             relay = over_cycle(relay, {2: ROW, 1: -ROW})
             relay = over_cycle(relay, {2: -1, 1: 1})
             relay = over_cycle(relay, {1: -1, 2: 1})

time: 432 us -> 398 us (0.921)
  waiting for transfers between devices: 256 us -> 232 us
  starting transfers between devices: 87.3 us -> 73 us
    ppermute x17, starting transfers between devices: 65.9 us -> 44.8 us  [exchange(): return lax.ppermute(value, 'gossip', pairs)]
    ppermute x6, waiting for transfers between devices: 15.2 us -> 6.39 us  [over_cycle(): return lax.ppermute(value, 'gossip', pairs)]
    ppermute x17, waiting for transfers between devices: 227 us -> 220 us  [exchange(): return lax.ppermute(value, 'gossip', pairs)]
    ppermute x6, starting transfers between devices: 13.2 us -> 20.1 us  [over_cycle(): return lax.ppermute(value, 'gossip', pairs)]
    ppermute x3, waiting for transfers between devices: 12.4 us -> 6.22 us  [other_chip(): return lax.ppermute(value, 'mp', [(s, s ^ 2) for s in range(count)])]
    unnamed x74 -> x72, local copies, waits for them, and re-layouts: 9.95 us -> 8.61 us
  transfers between devices with their start and end apart: 32 -> 31, of which waited for: 7 -> 7; matrix products, arithmetic and copies ran while one was open for 9% -> 10% of each run, Pallas kernels for 6% -> 7%
where the time goes in v4:
time: 398 us; the launch traced here: 397 us
  waiting for transfers between devices  232 us (58%)
  starting transfers between devices  73 us (18%)
  Pallas kernels  37.4 us (9%)
  matrix products  24.7 us (6%)
  other arithmetic  17.4 us (4%)
  local copies, waits for them, and re-layouts  10.6 us (3%)
    ppermute x17, waiting for transfers between devices, exchange(): return lax.ppermute(value, 'gossip', pairs)  220 us
    ppermute x17, starting transfers between devices, exchange(): return lax.ppermute(value, 'gossip', pairs)  44.8 us
    dot_general x14, matrix products, dot(): lax.dot_general(a, b, (dims, ((), ())), preferred_element_type=jnp.float32)  24.7 us
    pallas_call x5, Pallas kernels, mix_rows(): pl.pallas_call(body, grid=(rows // block,), in_specs=[piece] * 3 + [pl.Bl...  20.8 us
    ppermute x6, starting transfers between devices, over_cycle(): return lax.ppermute(value, 'gossip', pairs)  20.1 us
    pallas_call x1, Pallas kernels, forward(): pl.pallas_call(lambda *refs: forward_body(*refs, in_scale=in_scale), name...  8.92 us
    unnamed x72, local copies, waits for them, and re-layouts  8.61 us
  transfers between devices with their start and end apart: 31, of which 7 were waited for; matrix products, arithmetic and copies ran while one was open for 10% of the time, Pallas kernels for 7%

profile of v4, /device:TPU:0, one launch (start us, length us, event | category | flops | bytes accessed | tf_op | source)
XLA Modules:
  0.0 396.8 jit_solution(16875381620399808825)
XLA Ops:
  0.6 8.9 %forward.1 = (bf16[512,1024]{1,0:T(8,128)(2,1)}, bf16[512,384]{1,0:T(8,128)(2,1)}) custom-call(s32[1]{0:T(128)} %bitcast.2.refs_0_, bf16[512,2048]{1,0:T(8,128)(2,1)} %bitcast.131, bf16[2048,1024]{1,0:T(8,128)(2,1)} %bitcast.129, bf16[2048,1024]{1,0:T(8,128)(2,1)} %bitcast.127, bf16[1024,2048]{1,0:T(8,128)(2,1)} %bitcast.138), custom_call_target="tpu_custom_call" | custom-call | tf_op jit(solution)/shard_map/forward/pallas_call | solution.py:152
  9.6 3.6 convolution_convert_fusion
  13.7 3.5 fusion.15
  19.4 7.0 %slopes.1 = (bf16[512,1024]{1,0:T(8,128)(2,1)S(1)}, bf16[512,1024]{1,0:T(8,128)(2,1)S(1)}) custom-call(bf16[512,2048]{1,0:T(8,128)(2,1)S(1)} %bitcast.132, bf16[2048,1024]{1,0:T(8,128)(2,1)S(1)} %bitcast.130, bf16[2048,1024]{1,0:T(8,128)(2,1)S(1)} %bitcast.128), custom_call_target="tpu_custom_call" | custom-call | tf_op jit(solution)/shard_map/slopes/pallas_call | solution.py:183
  30.3 3.1 fusion.39
  34.7 3.4 collective-permute-start.1
  40.8 3.2 collective-permute-start.3
  44.1 4.3 %collective-permute-done.1 = bf16[512,384]{1,0:T(8,128)(2,1)S(1)} collective-permute-done((bf16[512,384]{1,0:T(8,128)(2,1)S(1)}, bf16[512,384]{1,0:T(8,128)(2,1)S(1)}, u32[]{:S(2)}, u32[]{:S(2)}) %collective-permute-start.1) | collective-permute-done | bytes 393248 | tf_op jit(solution)/shard_map/ppermute | solution.py:30
  53.8 5.3 %collective-permute-start.20 = (bf16[400,384]{1,0:T(8,128)(2,1)S(1)}, bf16[400,384]{1,0:T(8,128)(2,1)S(1)}, u32[]{:S(2)}, u32[]{:S(2)}) collective-permute-start(bf16[400,384]{1,0:T(8,128)(2,1)S(1)} %slice.91), channel_id=1, source_target_pairs={{0,4},{12,8},{16,20},{28,24},{32,36},{44,40},{48,52},{60,56},{64,6... | collective-permute-start | bytes 921608 | tf_op jit(solution)/shard_map/ppermute | solution.py:44
  68.6 7.4 %collective-permute-start.27 = (bf16[1024,128]{1,0:T(8,128)(2,1)S(1)}, bf16[1024,128]{1,0:T(8,128)(2,1)S(1)}, u32[]{:S(2)}, u32[]{:S(2)}) collective-permute-start(bf16[1024,128]{1,0:T(8,128)(2,1)S(1)} %fusion.22), channel_id=1, source_target_pairs={{0,124},{4,8},{8,4},{12,16},{16,12},{20,24},{24,20},{28,32},{32,28... | collective-permute-start | bytes 786440 | tf_op jit(solution)/shard_map/ppermute | solution.py:20
  78.8 13.1 %collective-permute-done.28 = bf16[1024,128]{1,0:T(8,128)(2,1)} collective-permute-done((bf16[1024,128]{1,0:T(8,128)(2,1)S(1)}, bf16[1024,128]{1,0:T(8,128)(2,1)}, u32[]{:S(2)}, u32[]{:S(2)}) %collective-permute-start.28) | collective-permute-done | bytes 262176 | tf_op jit(solution)/shard_map/ppermute | solution.py:20
  92.0 9.2 %collective-permute-start.24 = (bf16[624,384]{1,0:T(8,128)(2,1)S(1)}, bf16[624,384]{1,0:T(8,128)(2,1)S(1)}, u32[]{:S(2)}, u32[]{:S(2)}) collective-permute-start(bf16[624,384]{1,0:T(8,128)(2,1)S(1)} %slice.94), channel_id=1, source_target_pairs={{0,124},{12,16},{16,12},{28,32},{32,28},{44,48},{48,44},{60,64},{6... | collective-permute-start | bytes 1437704 | tf_op jit(solution)/shard_map/ppermute | solution.py:44
  105.5 6.4 %collective-permute-done.24 = bf16[624,384]{1,0:T(8,128)(2,1)S(1)} collective-permute-done((bf16[624,384]{1,0:T(8,128)(2,1)S(1)}, bf16[624,384]{1,0:T(8,128)(2,1)S(1)}, u32[]{:S(2)}, u32[]{:S(2)}) %collective-permute-start.24) | collective-permute-done | bytes 479264 | tf_op jit(solution)/shard_map/ppermute | solution.py:44
  111.9 6.0 %collective-permute-start.25 = (bf16[1024,512]{1,0:T(8,128)(2,1)}, bf16[1024,512]{1,0:T(8,128)(2,1)S(1)}, u32[]{:S(2)}, u32[]{:S(2)}) collective-permute-start(bf16[1024,512]{1,0:T(8,128)(2,1)} %fusion.4), channel_id=1, source_target_pairs={{0,124},{4,8},{8,4},{12,16},{16,12},{20,24},{24,20},{28,32},{32,28... | collective-permute-start | bytes 3145736 | tf_op jit(solution)/shard_map/ppermute | solution.py:20
  122.5 6.0 %collective-permute-start.8 = (bf16[2048,1024]{1,0:T(8,128)(2,1)S(1)}, bf16[2048,1024]{1,0:T(8,128)(2,1)S(1)}, u32[]{:S(2)}, u32[]{:S(2)}) collective-permute-start(bf16[2048,1024]{1,0:T(8,128)(2,1)S(1)} %fusion.own), channel_id=1, source_target_pairs={{0,124},{4,8},{8,4},{12,16},{16,12},{20,24},{24,20},{28,32},{32,28... | collective-permute-start | bytes 12582920 | tf_op jit(solution)/shard_map/ppermute | solution.py:20
  128.6 19.4 %collective-permute-done.14.lower = bf16[128,1024]{1,0:T(8,128)(2,1)S(1)} collective-permute-done((bf16[128,1024]{1,0:T(8,128)(2,1)S(1)}, bf16[128,1024]{1,0:T(8,128)(2,1)S(1)}, u32[]{:S(2)}, u32[]{:S(2)}) %collective-permute-start.14) | collective-permute-done | bytes 262176 | tf_op jit(solution)/shard_map/ppermute | solution.py:20
  152.5 6.0 %collective-permute-start.16 = (bf16[1792,1024]{1,0:T(8,128)(2,1)S(1)}, bf16[1792,1024]{1,0:T(8,128)(2,1)S(1)}, u32[]{:S(2)}, u32[]{:S(2)}) collective-permute-start(bf16[1792,1024]{1,0:T(8,128)(2,1)S(1)} %fusion.1.own), channel_id=1, source_target_pairs={{0,124},{4,8},{8,4},{12,16},{16,12},{20,24},{24,20},{28,32},{32,28... | collective-permute-start | bytes 11010056 | tf_op jit(solution)/shard_map/ppermute | solution.py:20
  158.5 127.8 %collective-permute-done.30 = bf16[1024,1024]{1,0:T(8,128)(2,1)S(1)} collective-permute-done((bf16[1024,1024]{1,0:T(8,128)(2,1)}, bf16[1024,1024]{1,0:T(8,128)(2,1)S(1)}, u32[]{:S(2)}, u32[]{:S(2)}) %collective-permute-start.30) | collective-permute-done | bytes 2097184 | tf_op jit(solution)/shard_map/ppermute | solution.py:20
  286.4 6.0 %collective-permute-start.29 = (bf16[1024,1024]{1,0:T(8,128)(2,1)}, bf16[1024,1024]{1,0:T(8,128)(2,1)}, u32[]{:S(2)}, u32[]{:S(2)}) collective-permute-start(bf16[1024,1024]{1,0:T(8,128)(2,1)} %subtract_convert_fusion), channel_id=1, source_target_pairs={{0,124},{4,8},{8,4},{12,16},{16,12},{20,24},{24,20},{28,32},{32,28... | collective-permute-start | bytes 6291464 | tf_op jit(solution)/shard_map/ppermute | solution.py:20
  300.3 59.4 %collective-permute-done.29 = bf16[1024,1024]{1,0:T(8,128)(2,1)} collective-permute-done((bf16[1024,1024]{1,0:T(8,128)(2,1)}, bf16[1024,1024]{1,0:T(8,128)(2,1)}, u32[]{:S(2)}, u32[]{:S(2)}) %collective-permute-start.29) | collective-permute-done | bytes 2097184 | tf_op jit(solution)/shard_map/ppermute | solution.py:20
  359.6 5.7 %collective-permute-start.10 = (bf16[64,1024]{1,0:T(8,128)(2,1)S(1)}, bf16[64,1024]{1,0:T(8,128)(2,1)S(1)}, u32[]{:S(2)}, u32[]{:S(2)}) collective-permute-start(bf16[64,1024]{1,0:T(8,128)(2,1)S(1)} %fusion.28.own), channel_id=1, source_target_pairs={{0,124},{4,8},{8,4},{12,16},{16,12},{20,24},{24,20},{28,32},{32,28... | collective-permute-start | bytes 393224 | tf_op jit(solution)/shard_map/ppermute | solution.py:20
  370.8 3.8 fusion.3
  374.6 10.1 %shard_map.76 = bf16[2048,1024]{1,0:T(8,128)(2,1)} custom-call(bf16[2048,1024]{1,0:T(8,128)(2,1)} %copy-done.16, bf16[2048,1024]{1,0:T(8,128)(2,1)} %copy-done.15, bf16[2048,1024]{1,0:T(8,128)(2,1)} %copy-done.17), custom_call_target="tpu_custom_call" | custom-call | tf_op jit(solution)/shard_map/pallas_call | solution.py:62
  386.0 8.5 %shard_map.77.rest_0_ = bf16[2048,1024]{1,0:T(8,128)(2,1)} custom-call(bf16[1792,1024]{1,0:T(8,128)(2,1)} %copy-done.19, bf16[1792,1024]{1,0:T(8,128)(2,1)} %copy-done.18, bf16[1792,1024]{1,0:T(8,128)(2,1)} %copy-done.20, bf16[16,1024]{1,0:T(8,128)(2,1)} %slice.90.rest_0_), custom_call_target="tpu_custom_call" | custom-call | tf_op jit(solution)/shard_map/pallas_call | solution.py:62
  (148 shorter events, 58.5 us)
Async XLA Ops:
  13.2 24.9 %collective-permute-start.2 = (bf16[512,640]{1,0:T(8,128)(2,1)}, bf16[512,640]{1,0:T(8,128)(2,1)}, u32[]{:S(2)}, u32[]{:S(2)}) collective-permute-start(bf16[512,640]{1,0:T(8,128)(2,1)} %convolution_convert_fusion), channel_id=1, source_target_pairs={{0,1},{1,0},{2,3},{3,2},{4,5},{5,4},{6,7},{7,6},{8,9},{9,8},{10,11... | collective-permute-start | bytes 1966088 | tf_op jit(solution)/shard_map/ppermute | solution.py:25
  13.2 20.2 %collective-permute-start = (bf16[512,384]{1,0:T(8,128)(2,1)}, bf16[512,384]{1,0:T(8,128)(2,1)S(1)}, u32[]{:S(2)}, u32[]{:S(2)}) collective-permute-start(bf16[512,384]{1,0:T(8,128)(2,1)} %get-tuple-element.10), channel_id=1, source_target_pairs={{0,1},{1,0},{2,3},{3,2},{4,5},{5,4},{6,7},{7,6},{8,9},{9,8},{10,11... | collective-permute-start | bytes 1179656 | tf_op jit(solution)/shard_map/ppermute | solution.py:25
  40.8 20.6 %collective-permute-start.3 = (bf16[512,512]{1,0:T(8,128)(2,1)S(1)}, bf16[512,512]{1,0:T(8,128)(2,1)S(1)}, u32[]{:S(2)}, u32[]{:S(2)}) collective-permute-start(bf16[512,512]{1,0:T(8,128)(2,1)S(1)} %fusion.44), channel_id=1, source_target_pairs={{0,2},{1,3},{2,0},{3,1},{4,6},{5,7},{6,4},{7,5},{8,10},{9,11},{10,... | collective-permute-start | bytes 1572872 | tf_op jit(solution)/shard_map/ppermute | solution.py:30
  50.6 67.7 %collective-permute-start.19 = (bf16[1024,384]{1,0:T(8,128)(2,1)S(1)}, bf16[1024,384]{1,0:T(8,128)(2,1)}, u32[]{:S(2)}, u32[]{:S(2)}) collective-permute-start(bf16[1024,384]{1,0:T(8,128)(2,1)S(1)} %subtract_convert_fusion.1), channel_id=1, source_target_pairs={{4,8},{8,4},{20,24},{24,20},{36,40},{40,36},{52,56},{56,52},{68,72... | collective-permute-start | bytes 2359304 | tf_op jit(solution)/shard_map/ppermute | solution.py:44
  53.8 22.2 %collective-permute-start.20 = (bf16[400,384]{1,0:T(8,128)(2,1)S(1)}, bf16[400,384]{1,0:T(8,128)(2,1)S(1)}, u32[]{:S(2)}, u32[]{:S(2)}) collective-permute-start(bf16[400,384]{1,0:T(8,128)(2,1)S(1)} %slice.91), channel_id=1, source_target_pairs={{0,4},{12,8},{16,20},{28,24},{32,36},{44,40},{48,52},{60,56},{64,6... | collective-permute-start | bytes 921608 | tf_op jit(solution)/shard_map/ppermute | solution.py:44
  66.2 56.3 %collective-permute-start.18 = (bf16[1024,384]{1,0:T(8,128)(2,1)S(1)}, bf16[1024,384]{1,0:T(8,128)(2,1)}, u32[]{:S(2)}, u32[]{:S(2)}) collective-permute-start(bf16[1024,384]{1,0:T(8,128)(2,1)S(1)} %subtract_convert_fusion.1), channel_id=1, source_target_pairs={{0,4},{4,0},{8,12},{12,8},{16,20},{20,16},{24,28},{28,24},{32,36},... | collective-permute-start | bytes 2359304 | tf_op jit(solution)/shard_map/ppermute | solution.py:20
  67.9 24.0 %collective-permute-start.28 = (bf16[1024,128]{1,0:T(8,128)(2,1)S(1)}, bf16[1024,128]{1,0:T(8,128)(2,1)}, u32[]{:S(2)}, u32[]{:S(2)}) collective-permute-start(bf16[1024,128]{1,0:T(8,128)(2,1)S(1)} %fusion.22), channel_id=1, source_target_pairs={{0,4},{4,0},{8,12},{12,8},{16,20},{20,16},{24,28},{28,24},{32,36},... | collective-permute-start | bytes 786440 | tf_op jit(solution)/shard_map/ppermute | solution.py:20
  68.6 36.8 %collective-permute-start.27 = (bf16[1024,128]{1,0:T(8,128)(2,1)S(1)}, bf16[1024,128]{1,0:T(8,128)(2,1)S(1)}, u32[]{:S(2)}, u32[]{:S(2)}) collective-permute-start(bf16[1024,128]{1,0:T(8,128)(2,1)S(1)} %fusion.22), channel_id=1, source_target_pairs={{0,124},{4,8},{8,4},{12,16},{16,12},{20,24},{24,20},{28,32},{32,28... | collective-permute-start | bytes 786440 | tf_op jit(solution)/shard_map/ppermute | solution.py:20
  76.0 25.2 %collective-permute-start.21 = (bf16[400,384]{1,0:T(8,128)(2,1)S(1)}, bf16[400,384]{1,0:T(8,128)(2,1)}, u32[]{:S(2)}, u32[]{:S(2)}) collective-permute-start(bf16[400,384]{1,0:T(8,128)(2,1)S(1)} %collective-permute-done.20), channel_id=1, source_target_pairs={{4,116},{8,24},{20,4},{24,40},{36,20},{40,56},{52,36},{56,72},{68,... | collective-permute-start | bytes 921608 | tf_op jit(solution)/shard_map/ppermute | solution.py:44
  105.4 47.0 %collective-permute-start.26 = (bf16[1024,512]{1,0:T(8,128)(2,1)}, bf16[1024,512]{1,0:T(8,128)(2,1)S(1)}, u32[]{:S(2)}, u32[]{:S(2)}) collective-permute-start(bf16[1024,512]{1,0:T(8,128)(2,1)} %fusion.4), channel_id=1, source_target_pairs={{0,4},{4,0},{8,12},{12,8},{16,20},{20,16},{24,28},{28,24},{32,36},... | collective-permute-start | bytes 3145736 | tf_op jit(solution)/shard_map/ppermute | solution.py:20
  111.9 46.6 %collective-permute-start.25 = (bf16[1024,512]{1,0:T(8,128)(2,1)}, bf16[1024,512]{1,0:T(8,128)(2,1)S(1)}, u32[]{:S(2)}, u32[]{:S(2)}) collective-permute-start(bf16[1024,512]{1,0:T(8,128)(2,1)} %fusion.4), channel_id=1, source_target_pairs={{0,124},{4,8},{8,4},{12,16},{16,12},{20,24},{24,20},{28,32},{32,28... | collective-permute-start | bytes 3145736 | tf_op jit(solution)/shard_map/ppermute | solution.py:20
  118.2 29.8 %collective-permute-start.14 = (bf16[128,1024]{1,0:T(8,128)(2,1)S(1)}, bf16[128,1024]{1,0:T(8,128)(2,1)S(1)}, u32[]{:S(2)}, u32[]{:S(2)}) collective-permute-start(bf16[128,1024]{1,0:T(8,128)(2,1)S(1)} %fusion.23.own), channel_id=1, source_target_pairs={{0,124},{4,8},{8,4},{12,16},{16,12},{20,24},{24,20},{28,32},{32,28... | collective-permute-start | bytes 786440 | tf_op jit(solution)/shard_map/ppermute | solution.py:20
  118.6 29.4 %collective-permute-start.23 = (bf16[400,384]{1,0:T(8,128)(2,1)}, bf16[400,384]{1,0:T(8,128)(2,1)S(1)}, u32[]{:S(2)}, u32[]{:S(2)}) collective-permute-start(bf16[400,384]{1,0:T(8,128)(2,1)} %collective-permute-done.22), channel_id=1, source_target_pairs={{4,0},{8,12},{20,16},{24,28},{36,32},{40,44},{52,48},{56,60},{68,6... | collective-permute-start | bytes 921608 | tf_op jit(solution)/shard_map/ppermute | solution.py:44
  122.5 243.5 %collective-permute-start.8 = (bf16[2048,1024]{1,0:T(8,128)(2,1)S(1)}, bf16[2048,1024]{1,0:T(8,128)(2,1)S(1)}, u32[]{:S(2)}, u32[]{:S(2)}) collective-permute-start(bf16[2048,1024]{1,0:T(8,128)(2,1)S(1)} %fusion.own), channel_id=1, source_target_pairs={{0,124},{4,8},{8,4},{12,16},{16,12},{20,24},{24,20},{28,32},{32,28... | collective-permute-start | bytes 12582920 | tf_op jit(solution)/shard_map/ppermute | solution.py:20
  148.0 219.5 %collective-permute-start.9 = (bf16[2048,1024]{1,0:T(8,128)(2,1)S(1)}, bf16[2048,1024]{1,0:T(8,128)(2,1)S(1)}, u32[]{:S(2)}, u32[]{:S(2)}) collective-permute-start(bf16[2048,1024]{1,0:T(8,128)(2,1)S(1)} %fusion.own), channel_id=1, source_target_pairs={{0,4},{4,0},{8,12},{12,8},{16,20},{20,16},{24,28},{28,24},{32,36},... | collective-permute-start | bytes 12582920 | tf_op jit(solution)/shard_map/ppermute | solution.py:20
  148.0 138.4 %collective-permute-start.30 = (bf16[1024,1024]{1,0:T(8,128)(2,1)}, bf16[1024,1024]{1,0:T(8,128)(2,1)S(1)}, u32[]{:S(2)}, u32[]{:S(2)}) collective-permute-start(bf16[1024,1024]{1,0:T(8,128)(2,1)} %subtract_convert_fusion), channel_id=1, source_target_pairs={{0,4},{4,0},{8,12},{12,8},{16,20},{20,16},{24,28},{28,24},{32,36},... | collective-permute-start | bytes 6291464 | tf_op jit(solution)/shard_map/ppermute | solution.py:20
  152.5 212.8 %collective-permute-start.16 = (bf16[1792,1024]{1,0:T(8,128)(2,1)S(1)}, bf16[1792,1024]{1,0:T(8,128)(2,1)S(1)}, u32[]{:S(2)}, u32[]{:S(2)}) collective-permute-start(bf16[1792,1024]{1,0:T(8,128)(2,1)S(1)} %fusion.1.own), channel_id=1, source_target_pairs={{0,124},{4,8},{8,4},{12,16},{16,12},{20,24},{24,20},{28,32},{32,28... | collective-permute-start | bytes 11010056 | tf_op jit(solution)/shard_map/ppermute | solution.py:20
  158.5 206.8 %collective-permute-start.17 = (bf16[1792,1024]{1,0:T(8,128)(2,1)S(1)}, bf16[1792,1024]{1,0:T(8,128)(2,1)S(1)}, u32[]{:S(2)}, u32[]{:S(2)}) collective-permute-start(bf16[1792,1024]{1,0:T(8,128)(2,1)S(1)} %fusion.1.own), channel_id=1, source_target_pairs={{0,4},{4,0},{8,12},{12,8},{16,20},{20,16},{24,28},{28,24},{32,36},... | collective-permute-start | bytes 11010056 | tf_op jit(solution)/shard_map/ppermute | solution.py:20
  286.4 73.3 %collective-permute-start.29 = (bf16[1024,1024]{1,0:T(8,128)(2,1)}, bf16[1024,1024]{1,0:T(8,128)(2,1)}, u32[]{:S(2)}, u32[]{:S(2)}) collective-permute-start(bf16[1024,1024]{1,0:T(8,128)(2,1)} %subtract_convert_fusion), channel_id=1, source_target_pairs={{0,124},{4,8},{8,4},{12,16},{16,12},{20,24},{24,20},{28,32},{32,28... | collective-permute-start | bytes 6291464 | tf_op jit(solution)/shard_map/ppermute | solution.py:20
  359.6 36.4 %collective-permute-start.10 = (bf16[64,1024]{1,0:T(8,128)(2,1)S(1)}, bf16[64,1024]{1,0:T(8,128)(2,1)S(1)}, u32[]{:S(2)}, u32[]{:S(2)}) collective-permute-start(bf16[64,1024]{1,0:T(8,128)(2,1)S(1)} %fusion.28.own), channel_id=1, source_target_pairs={{0,124},{4,8},{8,4},{12,16},{16,12},{20,24},{24,20},{28,32},{32,28... | collective-permute-start | bytes 393224 | tf_op jit(solution)/shard_map/ppermute | solution.py:20
  365.3 30.7 %collective-permute-start.11 = (bf16[64,1024]{1,0:T(8,128)(2,1)S(1)}, bf16[64,1024]{1,0:T(8,128)(2,1)S(1)}, u32[]{:S(2)}, u32[]{:S(2)}) collective-permute-start(bf16[64,1024]{1,0:T(8,128)(2,1)S(1)} %fusion.28.own), channel_id=1, source_target_pairs={{0,4},{4,0},{8,12},{12,8},{16,20},{20,16},{24,28},{28,24},{32,36},... | collective-permute-start | bytes 393224 | tf_op jit(solution)/shard_map/ppermute | solution.py:20
  365.3 30.0 %collective-permute-start.12 = (bf16[64,1024]{1,0:T(8,128)(2,1)S(1)}, bf16[64,1024]{1,0:T(8,128)(2,1)S(1)}, u32[]{:S(2)}, u32[]{:S(2)}) collective-permute-start(bf16[64,1024]{1,0:T(8,128)(2,1)S(1)} %fusion.29.own), channel_id=1, source_target_pairs={{0,124},{4,8},{8,4},{12,16},{16,12},{20,24},{24,20},{28,32},{32,28... | collective-permute-start | bytes 393224 | tf_op jit(solution)/shard_map/ppermute | solution.py:20
  366.0 29.3 %collective-permute-start.13 = (bf16[64,1024]{1,0:T(8,128)(2,1)S(1)}, bf16[64,1024]{1,0:T(8,128)(2,1)S(1)}, u32[]{:S(2)}, u32[]{:S(2)}) collective-permute-start(bf16[64,1024]{1,0:T(8,128)(2,1)S(1)} %fusion.29.own), channel_id=1, source_target_pairs={{0,4},{4,0},{8,12},{12,8},{16,20},{20,16},{24,28},{28,24},{32,36},... | collective-permute-start | bytes 393224 | tf_op jit(solution)/shard_map/ppermute | solution.py:20
  368.4 26.0 %collective-permute-start.15 = (bf16[128,1024]{1,0:T(8,128)(2,1)S(1)}, bf16[128,1024]{1,0:T(8,128)(2,1)S(1)}, u32[]{:S(2)}, u32[]{:S(2)}) collective-permute-start(bf16[128,1024]{1,0:T(8,128)(2,1)S(1)} %fusion.23.own), channel_id=1, source_target_pairs={{0,4},{4,0},{8,12},{12,8},{16,20},{20,16},{24,28},{28,24},{32,36},... | collective-permute-start | bytes 786440 | tf_op jit(solution)/shard_map/ppermute | solution.py:20
  (42 other events, 775.4 us)
